TPU v7x, 32 devices: a whole 2x2x4 slice. The times are simulated.
32 devices in a mesh: dp: 4 (over z), col: 2 (over y), fsdp: 4 (over x, core).
Axes of the slice: x: 2, y: 2, z: 4, core: 2. Of those that a mesh axis runs over, the one named last changes fastest.
Arguments:
- x_act: bfloat16 [98304, 576], P(('dp', 'col', 'fsdp'))
- dy_out: bfloat16 [98304, 576], P(('dp', 'col', 'fsdp'))
- w_gate: bfloat16 [576, 1536], P(None, ('col', 'fsdp'))
- w_up: bfloat16 [576, 1536], P(None, ('col', 'fsdp'))
- w_down: bfloat16 [1536, 576], P(('col', 'fsdp'))
- v_gate: bfloat16 [576, 1536], P(None, ('col', 'fsdp'))
- v_up: bfloat16 [576, 1536], P(None, ('col', 'fsdp'))
- v_down: bfloat16 [1536, 576], P(('col', 'fsdp'))
- g_next: float32 [32, 3, 576, 1536], P(('dp', 'col', 'fsdp'))
Outputs:
- output 1: bfloat16 [98304, 576], P(('dp', 'col', 'fsdp'))
- output 2: float32 [3, 576, 1536], P(None, None, ('col', 'fsdp'))
- output 3: float32 [32, 3, 576, 1536], P(('dp', 'col', 'fsdp'))
- output 4: bfloat16 [576, 1536], replicated
- output 5: bfloat16 [576, 1536], replicated
- output 6: bfloat16 [1536, 576], replicated
All inputs are finite; a program needn't handle non-finite values.
Results may differ from a plain program's by a relative error of at most 0.0105829.
Values are sent between devices in bfloat16 or wider.
A program may use at most 1 GiB of HBM per device.

v0:
```python
import jax
import jax.numpy as jnp
from jax import lax
from jax.sharding import PartitionSpec as P

ALL_AXES = ('dp', 'col', 'fsdp')
FSDP_AXES = ('col', 'fsdp')


def local_backward(x_loc, dy_loc, gate_full, up_full, down_full):
    pre_gate = jnp.dot(x_loc, gate_full, preferred_element_type=jnp.float32)
    pre_up = jnp.dot(x_loc, up_full, preferred_element_type=jnp.float32)
    sig_gate = jax.nn.sigmoid(pre_gate)
    act_gate = pre_gate * sig_gate
    hidden = (act_gate * pre_up).astype(jnp.bfloat16)
    d_hidden = jnp.einsum('td,fd->tf', dy_loc, down_full, preferred_element_type=jnp.float32)
    d_gate = (d_hidden * pre_up * sig_gate * (1.0 + pre_gate * (1.0 - sig_gate))).astype(jnp.bfloat16)
    d_up = (d_hidden * act_gate).astype(jnp.bfloat16)
    dx_loc = (jnp.einsum('tf,df->td', d_gate, gate_full, preferred_element_type=jnp.float32)
              + jnp.einsum('tf,df->td', d_up, up_full, preferred_element_type=jnp.float32)).astype(jnp.bfloat16)
    grad_local = jnp.stack([
        jnp.einsum('td,tf->df', x_loc, d_gate, preferred_element_type=jnp.float32),
        jnp.einsum('td,tf->df', x_loc, d_up, preferred_element_type=jnp.float32),
        jnp.einsum('td,tf->df', dy_loc, hidden, preferred_element_type=jnp.float32),
    ])
    return dx_loc, grad_local


def solution(mesh):
    def device_step(x_loc, dy_loc, w_gate, w_up, w_down, v_gate, v_up, v_down, g_next):
        gate_full = lax.all_gather(w_gate, FSDP_AXES, axis=1, tiled=True)
        up_full = lax.all_gather(w_up, FSDP_AXES, axis=1, tiled=True)
        down_full = lax.all_gather(w_down, FSDP_AXES, axis=0, tiled=True)
        v_gate_full = lax.all_gather(v_gate, FSDP_AXES, axis=1, tiled=True)
        v_up_full = lax.all_gather(v_up, FSDP_AXES, axis=1, tiled=True)
        v_down_full = lax.all_gather(v_down, FSDP_AXES, axis=0, tiled=True)
        grad_shard = lax.psum_scatter(g_next[0].astype(jnp.bfloat16), FSDP_AXES, scatter_dimension=2, tiled=True)
        grad_next = lax.psum(grad_shard.astype(jnp.float32), 'dp')
        dx_loc, grad_local = local_backward(x_loc, dy_loc, gate_full, up_full, down_full)
        return dx_loc, grad_next, grad_local[None], v_gate_full, v_up_full, v_down_full

    row_spec = P(ALL_AXES, None)
    col_shard = P(None, FSDP_AXES)
    row_shard = P(FSDP_AXES, None)
    dev_spec = P(ALL_AXES, None, None, None)
    return jax.shard_map(
        device_step, mesh=mesh,
        in_specs=(row_spec, row_spec, col_shard, col_shard, row_shard, col_shard, col_shard, row_shard, dev_spec),
        out_specs=(row_spec, P(None, None, FSDP_AXES), dev_spec, P(), P(), P()),
        check_vma=False)
```

profile of v0, /device:TPU:0, one launch (start us, length us, event | category | flops | bytes accessed | tf_op | source)
XLA Modules:
  0.0 310.3 jit_solution(17931733478260724727)
XLA Ops:
  7.2 0.7 all-gather.11.cloned.1.call-update
  8.0 0.7 all-gather.9.cloned.1.call-update
  8.7 0.7 all-gather.7.cloned.1.call-update
  10.0 0.5 all-gather.15.cloned.1.call-update
  11.2 10.5 %copy.19 = bf16[1,3,576,1536]{2,3,1,0:T(8,128)(2,1)} copy(f32[1,3,576,1536]{3,2,1,0:T(8,128)} %param.17) | data formatting | bytes 15925248 | tf_op args[8]
  21.7 17.9 %all-gather.11.cloned.1.call-done = bf16[576,1536]{0,1:T(8,128)(2,1)} async-done(((bf16[576,192]{0,1:T(8,128)(2,1)}), bf16[576,1536]{0,1:T(8,128)(2,1)}) %all-gather.11.cloned.1.call-update) | async-done | bytes 1769488 | tf_op jit(solution)/shard_map/all_gather | solution.py:31
  39.6 12.2 %fusion.6 = f32[3072,1536]{1,0:T(8,128)} fusion(bf16[3072,576]{0,1:T(8,128)(2,1)S(1)} %copy-done, bf16[576,1536]{0,1:T(8,128)(2,1)} %all-gather.11.cloned.1.call-done), kind=kOutput, calls=%fused_computation.14 | convolution fusion | flops 5435817984 | bytes 24182784 | tf_op jit(solution)/shard_map/dot_general | solution.py:11
  51.8 16.7 %all-gather.9.cloned.1.call-done = bf16[576,1536]{0,1:T(8,128)(2,1)} async-done(((bf16[576,192]{0,1:T(8,128)(2,1)}), bf16[576,1536]{0,1:T(8,128)(2,1)}) %all-gather.9.cloned.1.call-update) | async-done | bytes 1769488 | tf_op jit(solution)/shard_map/all_gather | solution.py:32
  68.5 12.3 %fusion.5 = f32[3072,1536]{1,0:T(8,128)} fusion(bf16[3072,576]{0,1:T(8,128)(2,1)S(1)} %copy-done, bf16[576,1536]{0,1:T(8,128)(2,1)} %all-gather.9.cloned.1.call-done), kind=kOutput, calls=%fused_computation.13 | convolution fusion | flops 5435817984 | bytes 24182784 | tf_op jit(solution)/shard_map/dot_general | solution.py:12
  80.8 16.6 %all-gather.7.cloned.1.call-done = bf16[1536,576]{1,0:T(8,128)(2,1)} async-done(((bf16[192,576]{1,0:T(8,128)(2,1)}), bf16[1536,576]{1,0:T(8,128)(2,1)}) %all-gather.7.cloned.1.call-update) | async-done | bytes 1769488 | tf_op jit(solution)/shard_map/all_gather | solution.py:33
  97.4 28.6 %multiply_convert_fusion.1 = (bf16[3072,1536]{1,0:T(8,128)(2,1)}, bf16[3072,1536]{1,0:T(8,128)(2,1)}) fusion(f32[3072,1536]{1,0:T(8,128)} %fusion.6, f32[3072,1536]{1,0:T(8,128)} %fusion.5, bf16[3072,576]{0,1:T(8,128)(2,1)} %param.10, bf16[1536,576]{1,0:T(8,128)(2,1)} %all-gather.7.cloned.1.call-done), kind=kOutput, calls=%fused_computation.1 | convolution fusion | flops 5497159680 | bytes 61931520 | tf_op jit(solution)/shard_map/td,fd->tf/dot_general | solution.py:16
  126.0 9.5 %convolution_bitcast_fusion = f32[1,576,1536]{2,1,0:T(8,128)} fusion(bf16[3072,576]{0,1:T(8,128)(2,1)S(1)} %copy-done, bf16[3072,1536]{1,0:T(8,128)(2,1)} %get-tuple-element.12), kind=kOutput, calls=%fused_computation.9 | convolution fusion | flops 5435817984 | bytes 16515072 | tf_op jit(solution)/shard_map/td,tf->df/dot_general | solution.py:23
  135.5 7.4 %convolution_bitcast_fusion.1 = f32[1,576,1536]{2,1,0:T(8,128)} fusion(bf16[3072,576]{0,1:T(8,128)(2,1)S(1)} %copy-done, bf16[3072,1536]{1,0:T(8,128)(2,1)S(1)} %copy-done.5), kind=kOutput, calls=%fused_computation.10 | convolution fusion | flops 5435817984 | bytes 16515072 | tf_op jit(solution)/shard_map/td,tf->df/dot_general | solution.py:22
  142.9 3.9 %copy.20 = bf16[576,1536]{1,0:T(8,128)(2,1)} copy(bf16[576,1536]{0,1:T(8,128)(2,1)} %all-gather.13.cloned.1.call-done) | data formatting | bytes 3538944
  146.8 8.1 %all-gather.15.cloned.1.call-done = bf16[576,1536]{0,1:T(8,128)(2,1)} async-done(((bf16[576,192]{0,1:T(8,128)(2,1)}), bf16[576,1536]{0,1:T(8,128)(2,1)}) %all-gather.15.cloned.1.call-update) | async-done | bytes 1769488 | tf_op jit(solution)/shard_map/all_gather | solution.py:35
  154.8 3.9 %copy.21 = bf16[576,1536]{1,0:T(8,128)(2,1)} copy(bf16[576,1536]{0,1:T(8,128)(2,1)} %all-gather.15.cloned.1.call-done) | data formatting | bytes 3538944
  158.7 24.9 %all-gather.17.cloned.1.call-done = bf16[1536,576]{1,0:T(8,128)(2,1)} async-done(((bf16[192,576]{1,0:T(8,128)(2,1)}), bf16[1536,576]{1,0:T(8,128)(2,1)}) %all-gather.17.cloned.1.call-update) | async-done | bytes 1769488 | tf_op jit(solution)/shard_map/all_gather | solution.py:36
  183.6 3.9 %copy.22 = bf16[1536,576]{0,1:T(8,128)(2,1)} copy(bf16[1536,576]{1,0:T(8,128)(2,1)} %all-gather.17.cloned.1.call-done) | data formatting | bytes 3538944
  187.5 17.8 %fusion.2 = f32[1,576,1536]{2,1,0:T(8,128)} fusion(bf16[3072,576]{0,1:T(8,128)(2,1)} %param.10, f32[3072,1536]{1,0:T(8,128)} %fusion.5, f32[3072,1536]{1,0:T(8,128)} %fusion.6), kind=kOutput, calls=%fused_computation.11 | convolution fusion | flops 5464129536 | bytes 44826624 | tf_op jit(solution)/shard_map/td,tf->df/dot_general | solution.py:24
  205.3 8.3 %maximum_bitcast_fusion = f32[1,3,576,1536]{3,2,1,0:T(8,128)} fusion(f32[1,576,1536]{2,1,0:T(8,128)} %fusion.2, f32[1,576,1536]{2,1,0:T(8,128)S(1)} %copy-done.2, f32[1,576,1536]{2,1,0:T(8,128)} %convolution_bitcast_fusion.1), kind=kLoop, calls=%fused_computation.5 | loop fusion | flops 5308416 | bytes 21233664 | tf_op jit(solution)/shard_map/broadcast_in_dim | solution.py:40
  213.6 8.4 %fusion.7 = f32[3072,576]{0,1:T(8,128)S(1)} fusion(bf16[3072,1536]{1,0:T(8,128)(2,1)} %get-tuple-element.13, bf16[576,1536]{0,1:T(8,128)(2,1)S(1)} %copy-done.3), kind=kOutput, calls=%fused_computation.15 | convolution fusion | flops 5435817984 | bytes 18284544 | tf_op jit(solution)/shard_map/tf,df->td/dot_general | solution.py:19
  222.1 10.0 %add_convert_fusion = bf16[3072,576]{0,1:T(8,128)(2,1)} fusion(f32[3072,576]{0,1:T(8,128)S(1)} %fusion.7, bf16[3072,1536]{1,0:T(8,128)(2,1)} %get-tuple-element.12, bf16[576,1536]{0,1:T(8,128)(2,1)S(1)} %copy-done.4), kind=kOutput, calls=%fused_computation.7 | convolution fusion | flops 5439356928 | bytes 21823488 | tf_op jit(solution)/shard_map/tf,df->td/dot_general | solution.py:20
  232.1 14.0 %reduce-scatter.2.cloned.1.call-done = bf16[3,576,192]{1,2,0:T(8,128)(2,1)} async-done(((bf16[3,576,1536]{1,2,0:T(8,128)(2,1)}), bf16[3,576,192]{1,2,0:T(8,128)(2,1)}) %reduce-scatter.2.cloned.1.call-update) | async-done | bytes 663568 | tf_op jit(solution)/shard_map/reduce_scatter | solution.py:37
  246.1 57.4 %all-reduce.1 = f32[3,576,192]{1,2,0:T(8,128)} all-reduce(bf16[3,576,192]{1,2,0:T(8,128)(2,1)} %reduce-scatter.2.cloned.1.call-done), channel_id=1, replica_groups=mesh['dp'=4,'col'=2,'fsdp'=4] {'dp'}, use_global_device_ids=true, to_apply=%region_1.0 | all-reduce | flops 331776 | bytes 1990656 | tf_op jit(solution)/shard_map/psum | solution.py:38
  (23 shorter events, 1.4 us)
Async XLA Ops:
  7.2 32.5 %copy-start = (bf16[3072,576]{0,1:T(8,128)(2,1)S(1)}, bf16[3072,576]{0,1:T(8,128)(2,1)}, u32[]{:S(2)}) copy-start(bf16[3072,576]{0,1:T(8,128)(2,1)} %param.9) | copy-start | bytes 10616836
  7.2 32.4 %all-gather.11.cloned.1.call-start = ((), (), s32[]{:S(2)}) async-start(), calls=%async_computation.3 | async-start | bytes 2211840 | tf_op jit(solution)/shard_map/all_gather | solution.py:31
  7.9 60.6 %all-gather.9.cloned.1.call-start = ((), (), s32[]{:S(2)}) async-start(), calls=%async_computation.2 | async-start | bytes 2211840 | tf_op jit(solution)/shard_map/all_gather | solution.py:32
  8.7 88.7 %all-gather.7.cloned.1.call-start = ((), (), s32[]{:S(2)}) async-start(), calls=%async_computation.1 | async-start | bytes 2211840 | tf_op jit(solution)/shard_map/all_gather | solution.py:33
  9.4 133.5 %all-gather.13.cloned.1.call-start = ((), (), s32[]{:S(2)}) async-start(), calls=%async_computation.5 | async-start | bytes 2211840 | tf_op jit(solution)/shard_map/all_gather | solution.py:34
  10.0 144.9 %all-gather.15.cloned.1.call-start = ((), (), s32[]{:S(2)}) async-start(), calls=%async_computation.6 | async-start | bytes 2211840 | tf_op jit(solution)/shard_map/all_gather | solution.py:35
  10.6 173.0 %all-gather.17.cloned.1.call-start = ((), (), s32[]{:S(2)}) async-start(), calls=%async_computation.7 | async-start | bytes 2211840 | tf_op jit(solution)/shard_map/all_gather | solution.py:36
  11.1 235.0 %reduce-scatter.2.cloned.1.call-start = ((), (), s32[]{:S(2)}) async-start(), calls=%async_computation.4 | async-start | bytes 6635520 | tf_op jit(solution)/shard_map/reduce_scatter | solution.py:37
  126.0 9.5 %copy-start.5 = (bf16[3072,1536]{1,0:T(8,128)(2,1)S(1)}, bf16[3072,1536]{1,0:T(8,128)(2,1)}, u32[]{:S(2)}) copy-start(bf16[3072,1536]{1,0:T(8,128)(2,1)} %get-tuple-element.13) | copy-start | bytes 28311556
  187.4 17.8 %copy-start.2 = (f32[1,576,1536]{2,1,0:T(8,128)S(1)}, f32[1,576,1536]{2,1,0:T(8,128)}, u32[]{:S(2)}) copy-start(f32[1,576,1536]{2,1,0:T(8,128)} %convolution_bitcast_fusion) | copy-start | bytes 10616836
  205.3 8.3 %copy-start.3 = (bf16[576,1536]{0,1:T(8,128)(2,1)S(1)}, bf16[576,1536]{0,1:T(8,128)(2,1)}, u32[]{:S(2)}) copy-start(bf16[576,1536]{0,1:T(8,128)(2,1)} %all-gather.11.cloned.1.call-done) | copy-start | bytes 5308420
  213.6 8.5 %copy-start.4 = (bf16[576,1536]{0,1:T(8,128)(2,1)S(1)}, bf16[576,1536]{0,1:T(8,128)(2,1)}, u32[]{:S(2)}) copy-start(bf16[576,1536]{0,1:T(8,128)(2,1)} %all-gather.9.cloned.1.call-done) | copy-start | bytes 5308420
  222.1 81.4 %copy-start.1 = (bf16[3072,576]{0,1:T(8,128)(2,1)S(1)}, bf16[3072,576]{0,1:T(8,128)(2,1)}, u32[]{:S(2)}) copy-start(bf16[3072,576]{0,1:T(8,128)(2,1)} %param.9) | copy-start | bytes 10616836
Sparse Core Ops, SparseCore 0:
  9.9 29.7 all-gather.10
  41.5 26.9 all-gather.8
  70.4 26.9 all-gather.6
  99.1 26.9 all-gather.12
  127.8 26.9 all-gather.14
  156.6 26.9 all-gather.16
  187.1 59.0 reduce-scatter.1
where the time goes:
time: 311 us; the launch traced here: 310 us
  matrix products  106 us (34%)
  waiting for transfers between devices  102 us (33%)
  blocking collectives  57.4 us (18%)
  local copies, waits for them, and re-layouts  22.1 us (7%)
  between operations  14.2 us (5%)
  other arithmetic  8.34 us (3%)
    psum x1, blocking collectives, device_step(): grad_next = lax.psum(grad_shard.astype(jnp.float32), 'dp')  57.4 us
    dot_general x1, matrix products, local_backward(): jnp.einsum('td,fd->tf', dy_loc, down_full, preferred_element_type=jnp.flo...  28.6 us
    all_gather x1, waiting for transfers between devices, device_step(): v_down_full = lax.all_gather(v_down, FSDP_AXES, axis=0, tiled=True)  24.9 us
    unnamed x16, local copies, waits for them, and re-layouts  22.1 us
    all_gather x1, waiting for transfers between devices, device_step(): gate_full = lax.all_gather(w_gate, FSDP_AXES, axis=1, tiled=True)  17.9 us
    dot_general x1, matrix products, local_backward(): jnp.einsum('td,tf->df', dy_loc, hidden, preferred_element_type=jnp.float32)  17.8 us
    all_gather x1, waiting for transfers between devices, device_step(): up_full = lax.all_gather(w_up, FSDP_AXES, axis=1, tiled=True)  16.7 us
    all_gather x1, waiting for transfers between devices, device_step(): down_full = lax.all_gather(w_down, FSDP_AXES, axis=0, tiled=True)  16.6 us
  transfers between devices with their start and end apart: 7, of which 6 were waited for; matrix products, arithmetic and copies ran while one was open for 44% of the time, Pallas kernels for 0%

commit v1 on v0

v1 whole, which is shorter than its diff:
```python
import functools

import jax
import jax.numpy as jnp
from jax import lax
from jax.experimental import pallas as pl
from jax.experimental.pallas import tpu as pltpu
from jax.sharding import PartitionSpec as P

ALL_AXES = ('dp', 'col', 'fsdp')
FSDP_AXES = ('col', 'fsdp')
MESH = pl.DeviceIdType.MESH

D = 576
F = 1536
N = 3072
T = 512
NT = N // T
SH = 192
FC = 384
RT = 144
HR = D // 2
QR = HR // 2
NN = (((1,), (0,)), ((), ()))
NTD = (((1,), (1,)), ((), ()))

STEPS = {
    'A': (0, 1, 2), 'W3': (15,), 'V': (3,),
    'B': (4, 6, 9), 'C': (8, 11, 13),
    'D0': (9, 12, 14), 'D1': (10, 13, 15), 'E0': (12, 15, 18), 'E1': (13, 16, 19),
    'V1': (20,), 'V2': (21,),
}


def dot(a, b, dn=NN):
    return lax.dot_general(a, b, dn, preferred_element_type=jnp.float32)


def kernel(xt, dyt, w1, w3, w2, v1, v3, v2, g, dxt, dw, vo, gs,
           xs, ys, pair, blk, vblk, wt, dxa, dwa, dab, hb, dxs,
           gf, gb, gp, r1, p2, r2, rr, z1, z2, zs, tt,
           s_tok, s_loc, s_g, s_dw, s_dx, s_vo, s_t, ss, rs):
    z = lax.axis_index('dp')
    y = lax.axis_index('col')
    f = lax.axis_index('fsdp')
    x = f // 2
    k = f % 2
    own = 2 * y + x
    partner = (z, y, f + 1 - 2 * k)
    xn = (z, y, (f + 2) % 4)
    yn = (z, 1 - y, f)
    z_pair = z + 1 - 2 * (z % 2)
    zp = (z_pair, y, f)
    zm = (3 - z, y, f)
    at_end = (z == 0) | (z == 3)
    inner = (z == 1) | (z == 2)

    def rcopy(n, src, dst, dev):
        return pltpu.make_async_remote_copy(
            src_ref=src, dst_ref=dst, send_sem=ss.at[n], recv_sem=rs.at[n], device_id=dev, device_id_type=MESH)

    def tok(t):
        cols = pl.ds(pl.multiple_of(t * T, T), T)
        return (pltpu.make_async_copy(xt.at[:, cols], xs.at[t], s_tok.at[0, t]),
                pltpu.make_async_copy(dyt.at[:, cols], ys.at[t], s_tok.at[1, t]))

    def gload(i, half):
        r0 = pl.multiple_of(half * (6 * RT) + i * RT, RT)
        return pltpu.make_async_copy(g.at[pl.ds(r0, RT), :], gf.at[i], s_g.at[i])

    shards = ((w1, w3, w2), (v1, v3, v2))
    myrows = pl.ds(pl.multiple_of(k * SH, SH), SH)
    local_shards = [pltpu.make_async_copy(shards[u][m], pair.at[u, m, myrows, :], s_loc.at[3 * u + m])
                    for u in range(2) for m in range(3)]
    for i in range(6):
        gload(i, 1 - k).start()
    for c in local_shards:
        c.start()

    bar = pltpu.get_barrier_semaphore()
    for dev in (partner, xn, yn, zp, zm):
        pl.semaphore_signal(bar, inc=1, device_id=dev, device_id_type=MESH)
    pl.semaphore_wait(bar, 5)

    to_pair = [rcopy(3 * u + m, shards[u][m], pair.at[u, m, myrows, :], partner) for u in range(2) for m in range(3)]
    half = pl.ds(pl.multiple_of(k * HR, HR), HR)
    other = pl.ds(pl.multiple_of((1 - k) * HR, HR), HR)
    qa = pl.ds(pl.multiple_of(k * HR, QR), QR)
    qb = pl.ds(pl.multiple_of(k * HR + QR, QR), QR)

    def blkcols(cx, cy):
        xx = 1 - x if cx else x
        yy = 1 - y if cy else y
        return pl.ds(pl.multiple_of((2 * yy + xx) * FC, FC), FC)

    w_x = rcopy(6, blk.at[0, :, half, :], blk.at[1, :, half, :], xn)
    w_y = rcopy(7, blk.at[0, :, half, :], blk.at[2, :, half, :], yn)
    w_f1 = rcopy(8, blk.at[1, :, half, :], blk.at[1, :, half, :], partner)
    w_f2 = rcopy(9, blk.at[2, :, half, :], blk.at[2, :, half, :], partner)
    w_da = rcopy(10, blk.at[1, :, qa, :], blk.at[3, :, qa, :], yn)
    w_db = rcopy(11, blk.at[2, :, qb, :], blk.at[3, :, qb, :], xn)
    w_f3 = rcopy(12, blk.at[3, :, half, :], blk.at[3, :, half, :], partner)

    v_own = pltpu.make_async_copy(vblk, vo.at[:, :, blkcols(0, 0)], s_vo)
    v_x = rcopy(13, vblk.at[:, half, :], vo.at[:, half, blkcols(0, 0)], xn)
    v_y = rcopy(14, vblk.at[:, half, :], vo.at[:, half, blkcols(0, 0)], yn)
    v_f1 = rcopy(15, vo.at[:, half, blkcols(1, 0)], vo.at[:, half, blkcols(1, 0)], partner)
    v_f2 = rcopy(16, vo.at[:, half, blkcols(0, 1)], vo.at[:, half, blkcols(0, 1)], partner)
    v_da = rcopy(17, vo.at[:, qa, blkcols(1, 0)], vo.at[:, qa, blkcols(1, 0)], yn)
    v_db = rcopy(18, vo.at[:, qb, blkcols(0, 1)], vo.at[:, qb, blkcols(0, 1)], xn)
    v_f3 = rcopy(19, vo.at[:, half, blkcols(1, 1)], vo.at[:, half, blkcols(1, 1)], partner)

    def to_partner(i):
        return rcopy(20 + i, gb.at[i], gp.at[i], partner)

    def first_x(j, yy):
        return rcopy(26 + 2 * j + yy, gp.at[j, 2 * yy + 1 - x], r1.at[j, yy], xn)

    def first_y(j, xx):
        return rcopy(32 + 2 * j + xx, gp.at[3 + j, 2 * (1 - y) + xx], r1.at[3 + j, xx], yn)

    def second_y(j):
        return rcopy(38 + j, p2.at[j, 1 - y], r2.at[j], yn)

    def second_x(j):
        return rcopy(41 + j, p2.at[3 + j, 1 - x], r2.at[3 + j], xn)

    def z_in(i):
        return rcopy(44 + i, rr.at[i], z1.at[i], zp)

    def z_mid(i):
        return rcopy(50 + i, zs.at[i], z2.at[i], zm)

    def z_out(i):
        return rcopy(56 + i, tt.at[i], tt.at[i], zp)

    def t_pair(i):
        return rcopy(62 + i, tt.at[i], gs.at[k, i], partner)

    def t_own(i):
        return pltpu.make_async_copy(tt.at[i], gs.at[k, i], s_t.at[i])

    for c in to_pair:
        c.start()
    for t in range(NT):
        for c in tok(t):
            c.start()

    def send_half(i, _):
        gload(i, 1 - k).wait()
        for q in range(4):
            gb[i, q] = gf[i, :, q * FC:(q + 1) * FC].astype(jnp.bfloat16)
        to_partner(i).start()
        gload(i, k).start()
        return 0

    lax.fori_loop(0, 6, send_half, 0)

    for m in range(3):
        local_shards[m].wait()
        to_pair[m].wait_recv()
        blk[0, m] = pair[0, m].T
    w_x.start()
    w_y.start()

    def own_tile(i):
        gload(i, k).wait()
        to_partner(i).wait_recv()
        for q in range(4):
            gp[i, q] = (gp[i, q].astype(jnp.float32)
                        + gf[i, :, q * FC:(q + 1) * FC].astype(jnp.bfloat16).astype(jnp.float32)).astype(jnp.bfloat16)

    def stage_a(j):
        own_tile(j)
        own_tile(3 + j)
        for b in range(2):
            first_x(j, b).start()
            first_y(j, b).start()

    def stage_b(j):
        for b in range(2):
            first_x(j, b).wait_recv()
            p2[j, b] = (gp[j, 2 * b + x].astype(jnp.float32) + r1[j, b].astype(jnp.float32)).astype(jnp.bfloat16)
            first_y(j, b).wait_recv()
            p2[3 + j, b] = (gp[3 + j, 2 * y + b].astype(jnp.float32)
                            + r1[3 + j, b].astype(jnp.float32)).astype(jnp.bfloat16)
        second_y(j).start()
        second_x(j).start()

    def stage_c(j):
        second_y(j).wait_recv()
        rr[j] = p2[j, y].astype(jnp.float32) + r2[j].astype(jnp.float32)
        second_x(j).wait_recv()
        rr[3 + j] = p2[3 + j, x].astype(jnp.float32) + r2[3 + j].astype(jnp.float32)

        @pl.when(at_end)
        def _():
            z_in(j).start()
            z_in(3 + j).start()

    def stage_d(i):
        @pl.when(inner)
        def _():
            z_in(i).wait_recv()
            zs[i] = rr[i] + z1[i]
            z_mid(i).start()

    def stage_e(i):
        @pl.when(inner)
        def _():
            z_mid(i).wait_recv()
            tt[i] = zs[i] + z2[i]
            z_out(i).start()
            t_pair(i).start()
            t_own(i).start()

    def v_start():
        for m in range(3):
            local_shards[3 + m].wait()
            to_pair[3 + m].wait_recv()
            vblk[m] = pair[1, m].T
        v_own.start()
        v_x.start()
        v_y.start()

    def w_1():
        w_x.wait_recv()
        w_f1.start()
        w_da.start()

    def w_2():
        w_y.wait_recv()
        w_f2.start()
        w_db.start()

    def w_3():
        w_da.wait_recv()
        w_db.wait_recv()
        w_f3.start()

    def v_1():
        v_x.wait_recv()
        v_f1.start()
        v_da.start()

    def v_2():
        v_y.wait_recv()
        v_f2.start()
        v_db.start()

    stages = {
        'A': stage_a, 'B': stage_b, 'C': stage_c,
        'D0': stage_d, 'D1': lambda j: stage_d(3 + j), 'E0': stage_e, 'E1': lambda j: stage_e(3 + j),
        'V': lambda j: v_start(), 'W3': lambda j: w_3(),
        'V1': lambda j: v_1(), 'V2': lambda j: v_2(),
    }
    order = ('W3', 'A', 'B', 'C', 'D0', 'D1', 'E0', 'E1', 'V', 'V1', 'V2')

    def tick(step):
        for name in order:
            for j, n in enumerate(STEPS[name]):
                if n < 24:
                    pl.when(step == n)(functools.partial(stages[name], j))

    def dw_out(c):
        cx, cy = c % 2, c // 2
        q = 2 * (y + cy - 2 * y * cy) + x + cx - 2 * x * cx
        return pltpu.make_async_copy(dwa, dw.at[:, :, pl.ds(pl.multiple_of(q * FC, FC), FC)], s_dw)

    def chunk(c, _):
        @pl.when(c == 1)
        def _():
            w_1()
            w_2()
            w_f1.wait_recv()

        @pl.when(c == 2)
        def _():
            w_f2.wait_recv()

        @pl.when(c == 3)
        def _():
            w_f3.wait_recv()

        for m in range(3):
            wt[m * FC:(m + 1) * FC, :] = blk[c, m].T

        @pl.when(c > 0)
        def _():
            dw_out(c - 1).wait()

        dwa[...] = jnp.zeros_like(dwa)

        def tile(t, _):
            step = c * NT + t

            @pl.when(c == 0)
            def _():
                for cp in tok(t):
                    cp.wait()
                dxa[t] = jnp.zeros((D, T), jnp.float32)

            tick(step)
            xv = xs[t]
            yv = ys[t]
            a = dot(wt[0:FC, :], xv)
            b = dot(wt[FC:2 * FC, :], xv)
            dh = dot(wt[2 * FC:3 * FC, :], yv)
            sg = jnp.tanh(a * 0.5) * 0.5 + 0.5
            act = a * sg
            hb[...] = (act * b).astype(jnp.bfloat16)
            dab[FC:, :] = (dh * act).astype(jnp.bfloat16)
            dab[:FC, :] = (dh * b * (sg + act * (1.0 - sg))).astype(jnp.bfloat16)
            dxa[t] += dot(blk[c, 0], dab[:FC, :]) + dot(blk[c, 1], dab[FC:, :])
            gw = dot(xv, dab[...], NTD)
            dwa[0] += gw[:, :FC]
            dwa[1] += gw[:, FC:]
            dwa[2] += dot(yv, hb[...], NTD)
            return 0

        lax.fori_loop(0, NT, tile, 0)
        dw_out(c).start()
        return 0

    lax.fori_loop(0, 4, chunk, 0)

    def dx_out(t):
        return pltpu.make_async_copy(dxs.at[t % 2], dxt.at[:, pl.ds(pl.multiple_of(t * T, T), T)], s_dx.at[t % 2])

    def write_dx(t, _):
        @pl.when(t >= 2)
        def _():
            dx_out(t - 2).wait()

        dxs[t % 2] = dxa[t].astype(jnp.bfloat16)
        dx_out(t).start()
        return 0

    lax.fori_loop(0, NT, write_dx, 0)

    for name in order:
        for j, n in enumerate(STEPS[name]):
            if n >= 24:
                stages[name](j)

    for i in range(6):
        @pl.when(at_end)
        def _():
            z_out(i).wait_recv()
            t_pair(i).start()
            t_own(i).start()
    v_da.wait_recv()
    v_db.wait_recv()
    v_f3.start()

    dw_out(3).wait()
    dx_out(NT - 2).wait()
    dx_out(NT - 1).wait()
    v_own.wait()
    for i in range(6):
        t_own(i).wait()
        t_pair(i).wait()
        to_partner(i).wait_send()

        @pl.when(at_end)
        def _():
            z_in(i).wait_send()

        @pl.when(inner)
        def _():
            z_mid(i).wait_send()
            z_out(i).wait_send()
    for j in range(3):
        for b in range(2):
            first_x(j, b).wait_send()
            first_y(j, b).wait_send()
        second_x(j).wait_send()
        second_y(j).wait_send()
    for c in to_pair:
        c.wait_send()
    for c in (w_x, w_y, w_f1, w_f2, w_da, w_db, w_f3, v_x, v_y, v_f1, v_f2, v_da, v_db, v_f3):
        c.wait_send()
    for c in (v_f1, v_f2, v_f3):
        c.wait_recv()


def step_kernel(xt, dyt, w1, w3, w2, v1, v3, v2, g):
    any_spec = pl.BlockSpec(memory_space=pl.ANY)
    bf, f32 = jnp.bfloat16, jnp.float32
    V = pltpu.VMEM
    dma = pltpu.SemaphoreType.DMA
    return pl.pallas_call(
        kernel,
        name='mlp_step',
        out_shape=(jax.ShapeDtypeStruct((D, N), bf), jax.ShapeDtypeStruct((3, D, F), f32),
                   jax.ShapeDtypeStruct((3, D, F), bf), jax.ShapeDtypeStruct((2, 6, RT, FC), f32)),
        in_specs=[any_spec] * 9,
        out_specs=(any_spec,) * 4,
        scratch_shapes=[
            V((NT, D, T), bf), V((NT, D, T), bf), V((2, 3, FC, D), bf), V((4, 3, D, FC), bf), V((3, D, FC), bf),
            V((3 * FC, D), bf), V((NT, D, T), f32), V((3, D, FC), f32), V((2 * FC, T), bf), V((FC, T), bf),
            V((2, D, T), bf),
            V((6, RT, F), f32), V((6, 4, RT, FC), bf), V((6, 4, RT, FC), bf), V((6, 2, RT, FC), bf),
            V((6, 2, RT, FC), bf), V((6, RT, FC), bf), V((6, RT, FC), f32), V((6, RT, FC), f32),
            V((6, RT, FC), f32), V((6, RT, FC), f32), V((6, RT, FC), f32),
            dma((2, NT)), dma((6,)), dma((6,)), dma, dma((2,)), dma, dma((6,)), dma((68,)), dma((68,)),
        ],
        compiler_params=pltpu.CompilerParams(
            collective_id=0, has_side_effects=True, vmem_limit_bytes=67_000_000),
        cost_estimate=pl.CostEstimate(flops=43_500_000_000, bytes_accessed=60_000_000, transcendentals=4_718_592),
    )(xt, dyt, w1, w3, w2, v1, v3, v2, g)


def solution(mesh):
    def device_step(x_loc, dy_loc, w_gate, w_up, w_down, v_gate, v_up, v_down, g_next):
        dxt, dw, vo, gs = step_kernel(
            x_loc.T, dy_loc.T, w_gate.T, w_up.T, w_down, v_gate.T, v_up.T, v_down, g_next.reshape(3 * D, F))
        core = lax.axis_index('fsdp') % 2
        grad = lax.dynamic_slice_in_dim(gs.reshape(3, D, FC), core * SH, SH, axis=2)
        return dxt.T, grad, dw[None], vo[0], vo[1], vo[2].T

    row_spec = P(ALL_AXES, None)
    col_shard = P(None, FSDP_AXES)
    row_shard = P(FSDP_AXES, None)
    dev_spec = P(ALL_AXES, None, None, None)
    return jax.shard_map(
        device_step, mesh=mesh,
        in_specs=(row_spec, row_spec, col_shard, col_shard, row_shard, col_shard, col_shard, row_shard, dev_spec),
        out_specs=(row_spec, P(None, None, FSDP_AXES), dev_spec, P(), P(), P()),
        check_vma=False)
```

time: 311 us -> 138 us (0.44)
  the two profiles are of different devices: /device:TPU:0 before, /device:TPU:9 now
where the time goes in v1:
time: 138 us
  Pallas kernels  117 us (85%)
  local copies, waits for them, and re-layouts  20.1 us (15%)
    pallas_call x1, Pallas kernels, step_kernel(): pl.pallas_call(kernel, name='mlp_step', out_shape=(jax.ShapeDtypeStruct((...  117 us
    unnamed x9, local copies, waits for them, and re-layouts  11.3 us
    transpose x1, local copies, waits for them, and re-layouts, device_step(): return (dxt.T, grad, dw[None], vo[0], vo[1], vo[2].T)  5.5 us
    dynamic_slice x1, local copies, waits for them, and re-layouts, device_step(): grad = lax.dynamic_slice_in_dim(gs.reshape(3, D, FC), core * SH, SH, axis=2)  3.37 us

profile of v1, /device:TPU:9, one launch (start us, length us, event | category | flops | bytes accessed | tf_op | source)
XLA Modules:
  0.0 138.3 jit_solution(7579964845375228970)
XLA Ops:
  0.7 117.5 %mlp_step.1 = (bf16[576,3072]{1,0:T(8,128)(2,1)}, f32[3,576,1536]{2,1,0:T(8,128)}, bf16[3,576,1536]{2,1,0:T(8,128)(2,1)}, f32[2,6,144,384]{3,2,1,0:T(8,128)}) custom-call(bf16[576,3072]{1,0:T(8,128)(2,1)} %bitcast.24, bf16[576,3072]{1,0:T(8,128)(2,1)} %bitcast.25, bf16[192,576]{1,0:T(8,128)(2,1)} %bitcast.26, bf16[192,576]{1,0:T(8,128)(2,1)} %bitcast.27, ...), custom_call_target="tpu_custom_call" | custom-call | flops 43499999232 | bytes 60000000 | tf_op jit(solution)/shard_map/mlp_step/pallas_call | solution.py:392
  118.1 0.0 slice-start
  118.2 3.4 %constant_dynamic-slice_fusion = f32[3,576,192]{2,1,0:T(8,128)} fusion(f32[3,576,384]{2,1,0:T(8,128)} %bitcast.22, s32[]{:T(128)S(6)} %select_n.11), kind=kLoop, calls=%fused_computation.3 | loop fusion | bytes 2654212 | tf_op jit(solution)/shard_map/dynamic_slice | solution.py:419
  121.5 2.6 %copy.16 = f32[3,576,192]{1,2,0:T(8,128)} copy(f32[3,576,192]{2,1,0:T(8,128)} %constant_dynamic-slice_fusion) | data formatting | bytes 2654208
  124.1 0.0 slice-start.1
  124.2 0.0 slice-start.2
  124.2 5.5 %slice_bitcast_fusion = (bf16[1536,576]{0,1:T(8,128)(2,1)}, bf16[576,1536]{1,0:T(8,128)(2,1)}, bf16[576,1536]{1,0:T(8,128)(2,1)}) fusion(bf16[3,576,1536]{2,1,0:T(8,128)(2,1)} %get-tuple-element.13), kind=kLoop, calls=%fused_computation | loop fusion | bytes 10616832 | tf_op jit(solution)/shard_map/transpose | solution.py:420
  129.7 4.5 %copy.19 = bf16[3072,576]{0,1:T(8,128)(2,1)} copy(bf16[3072,576]{0,1:T(8,128)(2,1)} %bitcast.21) | data formatting | bytes 7077888
  134.1 0.0 slice-done
  134.1 0.0 slice-done.1
  134.1 0.0 slice-done.2
  134.1 4.1 %copy.20 = f32[1,3,576,1536]{3,2,1,0:T(8,128)} copy(f32[1,3,576,1536]{3,2,1,0:T(8,128)S(1)} %bitcast.20) | data formatting | bytes 21233664
  (1 shorter events, 0.0 us)
Async XLA Ops:
  118.1 16.0 %slice-start = ((s8[10616832]{0:T(1024)(128)(4,1)}), s8[2228224]{0:T(1024)(128)(4,1)S(1)}, s32[]{:S(2)}) async-start(s8[10616832]{0:T(1024)(128)(4,1)} %bitcast.18), calls=%async_computation | async-start | bytes 4456448
  124.1 10.0 %slice-start.1 = ((s8[10616832]{0:T(1024)(128)(4,1)}), s8[4194304]{0:T(1024)(128)(4,1)S(1)}, s32[]{:S(2)}) async-start(s8[10616832]{0:T(1024)(128)(4,1)} %bitcast.18), calls=%async_computation.1 | async-start | bytes 8388608
  124.2 10.0 %slice-start.2 = ((s8[10616832]{0:T(1024)(128)(4,1)}), s8[4194304]{0:T(1024)(128)(4,1)S(1)}, s32[]{:S(2)}) async-start(s8[10616832]{0:T(1024)(128)(4,1)} %bitcast.18), calls=%async_computation.2 | async-start | bytes 8388608

commit v2 on v1

--- a/solution.py
+++ b/solution.py
@@ -25,10 +25,9 @@
 NTD = (((1,), (1,)), ((), ()))
 
 STEPS = {
-    'A': (0, 1, 2), 'W3': (15,), 'V': (3,),
-    'B': (4, 6, 9), 'C': (8, 11, 13),
-    'D0': (9, 12, 14), 'D1': (10, 13, 15), 'E0': (12, 15, 18), 'E1': (13, 16, 19),
-    'V1': (20,), 'V2': (21,),
+    'A': (0, 1, 6), 'W1': (4,), 'WZ': (9,), 'WD': (12,), 'W3': (16,), 'V': (13,), 'V1': (20, 22, 24),
+    'B': (6, 7, 10), 'C': (8, 11, 12),
+    'D0': (10, 14, 17), 'D1': (12, 16, 19), 'E0': (14, 18, 22), 'E1': (16, 20, 24),
 }
 
 
@@ -38,7 +37,7 @@
 
 def kernel(xt, dyt, w1, w3, w2, v1, v3, v2, g, dxt, dw, vo, gs,
            xs, ys, pair, blk, vblk, wt, dxa, dwa, dab, hb, dxs,
-           gf, gb, gp, r1, p2, r2, rr, z1, z2, zs, tt,
+           gf, gb, gp, r1, p2, r2, rb, z1, z2, zs, tt, to,
            s_tok, s_loc, s_g, s_dw, s_dx, s_vo, s_t, ss, rs):
     z = lax.axis_index('dp')
     y = lax.axis_index('col')
@@ -93,22 +92,32 @@
         yy = 1 - y if cy else y
         return pl.ds(pl.multiple_of((2 * yy + xx) * FC, FC), FC)
 
-    w_x = rcopy(6, blk.at[0, :, half, :], blk.at[1, :, half, :], xn)
-    w_y = rcopy(7, blk.at[0, :, half, :], blk.at[2, :, half, :], yn)
-    w_f1 = rcopy(8, blk.at[1, :, half, :], blk.at[1, :, half, :], partner)
-    w_f2 = rcopy(9, blk.at[2, :, half, :], blk.at[2, :, half, :], partner)
+    zo = z % 2
+    qm = pl.ds(pl.multiple_of(k * HR + zo * QR, QR), QR)
+    qo = pl.ds(pl.multiple_of(k * HR + (1 - zo) * QR, QR), QR)
+    w_x = rcopy(6, blk.at[0, :, qm, :], blk.at[1, :, qm, :], xn)
+    w_y = rcopy(7, blk.at[0, :, qm, :], blk.at[2, :, qm, :], yn)
+    w_zx = rcopy(8, blk.at[1, :, qm, :], blk.at[1, :, qm, :], zp)
+    w_zy = rcopy(9, blk.at[2, :, qm, :], blk.at[2, :, qm, :], zp)
+    w_f1a = rcopy(62, blk.at[1, :, qm, :], blk.at[1, :, qm, :], partner)
+    w_f1b = rcopy(63, blk.at[1, :, qo, :], blk.at[1, :, qo, :], partner)
+    w_f2a = rcopy(64, blk.at[2, :, qm, :], blk.at[2, :, qm, :], partner)
+    w_f2b = rcopy(65, blk.at[2, :, qo, :], blk.at[2, :, qo, :], partner)
     w_da = rcopy(10, blk.at[1, :, qa, :], blk.at[3, :, qa, :], yn)
     w_db = rcopy(11, blk.at[2, :, qb, :], blk.at[3, :, qb, :], xn)
     w_f3 = rcopy(12, blk.at[3, :, half, :], blk.at[3, :, half, :], partner)
 
     v_own = pltpu.make_async_copy(vblk, vo.at[:, :, blkcols(0, 0)], s_vo)
-    v_x = rcopy(13, vblk.at[:, half, :], vo.at[:, half, blkcols(0, 0)], xn)
-    v_y = rcopy(14, vblk.at[:, half, :], vo.at[:, half, blkcols(0, 0)], yn)
-    v_f1 = rcopy(15, vo.at[:, half, blkcols(1, 0)], vo.at[:, half, blkcols(1, 0)], partner)
-    v_f2 = rcopy(16, vo.at[:, half, blkcols(0, 1)], vo.at[:, half, blkcols(0, 1)], partner)
-    v_da = rcopy(17, vo.at[:, qa, blkcols(1, 0)], vo.at[:, qa, blkcols(1, 0)], yn)
-    v_db = rcopy(18, vo.at[:, qb, blkcols(0, 1)], vo.at[:, qb, blkcols(0, 1)], xn)
-    v_f3 = rcopy(19, vo.at[:, half, blkcols(1, 1)], vo.at[:, half, blkcols(1, 1)], partner)
+    def v_copies(m):
+        n = 66 + 7 * m
+        q0, q1, q2, q3 = blkcols(0, 0), blkcols(1, 0), blkcols(0, 1), blkcols(1, 1)
+        return (rcopy(n, vblk.at[m, half, :], vo.at[m, half, q0], xn),
+                rcopy(n + 1, vblk.at[m, half, :], vo.at[m, half, q0], yn),
+                rcopy(n + 2, vo.at[m, half, q1], vo.at[m, half, q1], partner),
+                rcopy(n + 3, vo.at[m, half, q2], vo.at[m, half, q2], partner),
+                rcopy(n + 4, vo.at[m, qa, q1], vo.at[m, qa, q1], yn),
+                rcopy(n + 5, vo.at[m, qb, q2], vo.at[m, qb, q2], xn),
+                rcopy(n + 6, vo.at[m, half, q3], vo.at[m, half, q3], partner))
 
     def to_partner(i):
         return rcopy(20 + i, gb.at[i], gp.at[i], partner)
@@ -126,19 +135,16 @@
         return rcopy(41 + j, p2.at[3 + j, 1 - x], r2.at[3 + j], xn)
 
     def z_in(i):
-        return rcopy(44 + i, rr.at[i], z1.at[i], zp)
+        return rcopy(44 + i, rb.at[i], z1.at[i], zp)
 
     def z_mid(i):
         return rcopy(50 + i, zs.at[i], z2.at[i], zm)
 
     def z_out(i):
-        return rcopy(56 + i, tt.at[i], tt.at[i], zp)
+        return rcopy(56 + i, tt.at[k, i], tt.at[k, i], zp)
 
     def t_pair(i):
-        return rcopy(62 + i, tt.at[i], gs.at[k, i], partner)
-
-    def t_own(i):
-        return pltpu.make_async_copy(tt.at[i], gs.at[k, i], s_t.at[i])
+        return rcopy(87 + i, tt.at[k, i], tt.at[k, i], partner)
 
     for c in to_pair:
         c.start()
@@ -187,50 +193,59 @@
         second_y(j).start()
         second_x(j).start()
 
+    def second(i):
+        return second_y(i) if i < 3 else second_x(i - 3)
+
+    def mine(i):
+        return y if i < 3 else x
+
     def stage_c(j):
-        second_y(j).wait_recv()
-        rr[j] = p2[j, y].astype(jnp.float32) + r2[j].astype(jnp.float32)
-        second_x(j).wait_recv()
-        rr[3 + j] = p2[3 + j, x].astype(jnp.float32) + r2[3 + j].astype(jnp.float32)
-
         @pl.when(at_end)
         def _():
-            z_in(j).start()
-            z_in(3 + j).start()
+            for i in (j, 3 + j):
+                second(i).wait_recv()
+                rb[i] = (p2[i, mine(i)].astype(jnp.float32) + r2[i].astype(jnp.float32)).astype(jnp.bfloat16)
+                z_in(i).start()
 
     def stage_d(i):
         @pl.when(inner)
         def _():
+            second(i).wait_recv()
             z_in(i).wait_recv()
-            zs[i] = rr[i] + z1[i]
+            zs[i] = (p2[i, mine(i)].astype(jnp.float32) + r2[i].astype(jnp.float32)) + z1[i].astype(jnp.float32)
             z_mid(i).start()
 
     def stage_e(i):
         @pl.when(inner)
         def _():
             z_mid(i).wait_recv()
-            tt[i] = zs[i] + z2[i]
+            tt[k, i] = zs[i] + z2[i]
             z_out(i).start()
             t_pair(i).start()
-            t_own(i).start()
 
     def v_start():
         for m in range(3):
             local_shards[3 + m].wait()
             to_pair[3 + m].wait_recv()
             vblk[m] = pair[1, m].T
+            v_copies(m)[0].start()
+            v_copies(m)[1].start()
         v_own.start()
-        v_x.start()
-        v_y.start()
 
     def w_1():
         w_x.wait_recv()
-        w_f1.start()
+        w_zx.start()
+        w_f1a.start()
+        w_y.wait_recv()
+        w_zy.start()
+        w_f2a.start()
+
+    def w_z():
+        w_zy.wait_recv()
+        w_f2b.start()
+
+    def w_d():
         w_da.start()
-
-    def w_2():
-        w_y.wait_recv()
-        w_f2.start()
         w_db.start()
 
     def w_3():
@@ -238,23 +253,28 @@
         w_db.wait_recv()
         w_f3.start()
 
-    def v_1():
+    def v_1(m):
+        v_x, v_y, v_f1, v_f2, v_da, v_db, _ = v_copies(m)
         v_x.wait_recv()
+        v_da.start()
         v_f1.start()
-        v_da.start()
-
-    def v_2():
         v_y.wait_recv()
+        v_db.start()
         v_f2.start()
-        v_db.start()
+
+    def v_2(m):
+        v_da, v_db, v_f3 = v_copies(m)[4:]
+        v_da.wait_recv()
+        v_db.wait_recv()
+        v_f3.start()
 
     stages = {
         'A': stage_a, 'B': stage_b, 'C': stage_c,
         'D0': stage_d, 'D1': lambda j: stage_d(3 + j), 'E0': stage_e, 'E1': lambda j: stage_e(3 + j),
-        'V': lambda j: v_start(), 'W3': lambda j: w_3(),
-        'V1': lambda j: v_1(), 'V2': lambda j: v_2(),
+        'V': lambda j: v_start(), 'V1': v_1,
+        'W1': lambda j: w_1(), 'WZ': lambda j: w_z(), 'WD': lambda j: w_d(), 'W3': lambda j: w_3(),
     }
-    order = ('W3', 'A', 'B', 'C', 'D0', 'D1', 'E0', 'E1', 'V', 'V1', 'V2')
+    order = ('W1', 'WZ', 'W3', 'B', 'A', 'C', 'D0', 'D1', 'E0', 'E1', 'WD', 'V', 'V1')
 
     def tick(step):
         for name in order:
@@ -270,13 +290,15 @@
     def chunk(c, _):
         @pl.when(c == 1)
         def _():
-            w_1()
-            w_2()
-            w_f1.wait_recv()
+            w_zx.wait_recv()
+            w_f1b.start()
+            w_f1a.wait_recv()
+            w_f1b.wait_recv()
 
         @pl.when(c == 2)
         def _():
-            w_f2.wait_recv()
+            w_f2a.wait_recv()
+            w_f2b.wait_recv()
 
         @pl.when(c == 3)
         def _():
@@ -343,23 +365,31 @@
             if n >= 24:
                 stages[name](j)
 
-    for i in range(6):
+    for m in range(3):
+        v_2(m)
+    for i in (0, 3, 1, 4, 2, 5):
         @pl.when(at_end)
         def _():
             z_out(i).wait_recv()
             t_pair(i).start()
-            t_own(i).start()
-    v_da.wait_recv()
-    v_db.wait_recv()
-    v_f3.start()
+    for i in range(6):
+        t_pair(i).wait_recv()
+
+    def t_out(m):
+        return pltpu.make_async_copy(to.at[m, pl.ds(pl.multiple_of(k * SH, SH), SH), :], gs.at[m], s_t.at[m])
+
+    for m in range(3):
+        to[m] = jnp.concatenate([tt[(4 * m + r) // 6, (4 * m + r) % 6] for r in range(4)], axis=0).T
+        t_out(m).start()
 
     dw_out(3).wait()
     dx_out(NT - 2).wait()
     dx_out(NT - 1).wait()
     v_own.wait()
+    for m in range(3):
+        t_out(m).wait()
     for i in range(6):
-        t_own(i).wait()
-        t_pair(i).wait()
+        t_pair(i).wait_send()
         to_partner(i).wait_send()
 
         @pl.when(at_end)
@@ -378,10 +408,13 @@
         second_y(j).wait_send()
     for c in to_pair:
         c.wait_send()
-    for c in (w_x, w_y, w_f1, w_f2, w_da, w_db, w_f3, v_x, v_y, v_f1, v_f2, v_da, v_db, v_f3):
+    for c in (w_x, w_y, w_zx, w_zy, w_f1a, w_f1b, w_f2a, w_f2b, w_da, w_db, w_f3):
         c.wait_send()
-    for c in (v_f1, v_f2, v_f3):
-        c.wait_recv()
+    for m in range(3):
+        for c in v_copies(m):
+            c.wait_send()
+        for c in (v_copies(m)[2], v_copies(m)[3], v_copies(m)[6]):
+            c.wait_recv()
 
 
 def step_kernel(xt, dyt, w1, w3, w2, v1, v3, v2, g):
@@ -393,7 +426,7 @@
         kernel,
         name='mlp_step',
         out_shape=(jax.ShapeDtypeStruct((D, N), bf), jax.ShapeDtypeStruct((3, D, F), f32),
-                   jax.ShapeDtypeStruct((3, D, F), bf), jax.ShapeDtypeStruct((2, 6, RT, FC), f32)),
+                   jax.ShapeDtypeStruct((3, D, F), bf), jax.ShapeDtypeStruct((3, SH, D), f32)),
         in_specs=[any_spec] * 9,
         out_specs=(any_spec,) * 4,
         scratch_shapes=[
@@ -401,9 +434,9 @@
             V((3 * FC, D), bf), V((NT, D, T), f32), V((3, D, FC), f32), V((2 * FC, T), bf), V((FC, T), bf),
             V((2, D, T), bf),
             V((6, RT, F), f32), V((6, 4, RT, FC), bf), V((6, 4, RT, FC), bf), V((6, 2, RT, FC), bf),
-            V((6, 2, RT, FC), bf), V((6, RT, FC), bf), V((6, RT, FC), f32), V((6, RT, FC), f32),
-            V((6, RT, FC), f32), V((6, RT, FC), f32), V((6, RT, FC), f32),
-            dma((2, NT)), dma((6,)), dma((6,)), dma, dma((2,)), dma, dma((6,)), dma((68,)), dma((68,)),
+            V((6, 2, RT, FC), bf), V((6, RT, FC), bf), V((6, RT, FC), bf), V((6, RT, FC), bf),
+            V((6, RT, FC), f32), V((6, RT, FC), f32), V((2, 6, RT, FC), f32), V((3, FC, D), f32),
+            dma((2, NT)), dma((6,)), dma((6,)), dma, dma((2,)), dma, dma((3,)), dma((93,)), dma((93,)),
         ],
         compiler_params=pltpu.CompilerParams(
             collective_id=0, has_side_effects=True, vmem_limit_bytes=67_000_000),
@@ -415,9 +448,7 @@
     def device_step(x_loc, dy_loc, w_gate, w_up, w_down, v_gate, v_up, v_down, g_next):
         dxt, dw, vo, gs = step_kernel(
             x_loc.T, dy_loc.T, w_gate.T, w_up.T, w_down, v_gate.T, v_up.T, v_down, g_next.reshape(3 * D, F))
-        core = lax.axis_index('fsdp') % 2
-        grad = lax.dynamic_slice_in_dim(gs.reshape(3, D, FC), core * SH, SH, axis=2)
-        return dxt.T, grad, dw[None], vo[0], vo[1], vo[2].T
+        return dxt.T, gs.transpose(0, 2, 1), dw[None], vo[0], vo[1], vo[2].T
 
     row_spec = P(ALL_AXES, None)
     col_shard = P(None, FSDP_AXES)

time: 138 us -> 121 us (0.88)
  the two profiles are of different devices: /device:TPU:9 before, /device:TPU:0 now
where the time goes in v2:
time: 121 us; the launch traced here: 120 us
  Pallas kernels  104 us (86%)
  local copies, waits for them, and re-layouts  15.5 us (13%)
    pallas_call x1, Pallas kernels, step_kernel(): pl.pallas_call(kernel, name='mlp_step', out_shape=(jax.ShapeDtypeStruct((...  104 us
    unnamed x11, local copies, waits for them, and re-layouts  10 us
    transpose x1, local copies, waits for them, and re-layouts, device_step(): return (dxt.T, gs.transpose(0, 2, 1), dw[None], vo[0], vo[1], vo[2].T)  5.5 us

profile of v2, /device:TPU:0, one launch (start us, length us, event | category | flops | bytes accessed | tf_op | source)
XLA Modules:
  0.0 119.9 jit_solution(7932518622465691274)
XLA Ops:
  0.6 103.7 %mlp_step.1 = (bf16[576,3072]{1,0:T(8,128)(2,1)}, f32[3,576,1536]{2,1,0:T(8,128)}, bf16[3,576,1536]{2,1,0:T(8,128)(2,1)}, f32[3,192,576]{2,1,0:T(8,128)}) custom-call(bf16[576,3072]{1,0:T(8,128)(2,1)} %bitcast.24, bf16[576,3072]{1,0:T(8,128)(2,1)} %bitcast.25, bf16[192,576]{1,0:T(8,128)(2,1)} %bitcast.26, bf16[192,576]{1,0:T(8,128)(2,1)} %bitcast.27, ...), custom_call_target="tpu_custom_call" | custom-call | flops 43499999232 | bytes 60000000 | tf_op jit(solution)/shard_map/mlp_step/pallas_call | solution.py:425
  104.3 0.0 slice-start
  104.3 0.0 slice-start.1
  104.3 5.5 %slice_bitcast_fusion = (bf16[1536,576]{0,1:T(8,128)(2,1)}, bf16[576,1536]{1,0:T(8,128)(2,1)}, bf16[576,1536]{1,0:T(8,128)(2,1)}) fusion(bf16[3,576,1536]{2,1,0:T(8,128)(2,1)} %get-tuple-element.13), kind=kLoop, calls=%fused_computation | loop fusion | bytes 10616832 | tf_op jit(solution)/shard_map/transpose | solution.py:451
  109.8 0.0 copy-start
  109.8 0.0 slice-start.2
  109.9 4.7 %copy.18 = bf16[3072,576]{0,1:T(8,128)(2,1)} copy(bf16[3072,576]{0,1:T(8,128)(2,1)} %bitcast.21) | data formatting | bytes 7077888
  114.6 0.0 copy-done
  114.6 1.1 copy.19
  115.7 0.0 slice-done
  115.7 0.0 slice-done.1
  115.7 0.0 slice-done.2
  115.7 4.1 %copy.20 = f32[1,3,576,1536]{3,2,1,0:T(8,128)} copy(f32[1,3,576,1536]{3,2,1,0:T(8,128)S(1)} %bitcast.20) | data formatting | bytes 21233664
  (1 shorter events, 0.0 us)
Async XLA Ops:
  104.3 11.4 %slice-start = ((s8[10616832]{0:T(1024)(128)(4,1)}), s8[4194304]{0:T(1024)(128)(4,1)S(1)}, s32[]{:S(2)}) async-start(s8[10616832]{0:T(1024)(128)(4,1)} %bitcast.18), calls=%async_computation | async-start | bytes 8388608
  104.3 11.4 %slice-start.1 = ((s8[10616832]{0:T(1024)(128)(4,1)}), s8[4194304]{0:T(1024)(128)(4,1)S(1)}, s32[]{:S(2)}) async-start(s8[10616832]{0:T(1024)(128)(4,1)} %bitcast.18), calls=%async_computation.1 | async-start | bytes 8388608
  109.8 4.8 %copy-start = (f32[3,192,576]{2,1,0:T(8,128)S(1)}, f32[3,192,576]{2,1,0:T(8,128)}, u32[]{:S(2)}) copy-start(f32[3,192,576]{2,1,0:T(8,128)} %get-tuple-element.11) | copy-start | bytes 3981316
  109.8 5.9 %slice-start.2 = ((s8[10616832]{0:T(1024)(128)(4,1)}), s8[2228224]{0:T(1024)(128)(4,1)S(1)}, s32[]{:S(2)}) async-start(s8[10616832]{0:T(1024)(128)(4,1)} %bitcast.18), calls=%async_computation.2 | async-start | bytes 4456448

commit v3 on v2

--- a/solution.py
+++ b/solution.py
@@ -36,7 +36,7 @@
 
 
 def kernel(xt, dyt, w1, w3, w2, v1, v3, v2, g, dxt, dw, vo, gs,
-           xs, ys, pair, blk, vblk, wt, dxa, dwa, dab, hb, dxs,
+           xs, ys, pair, blk, vblk, wt, dxa, dwa, dab0, hb0, dab1, hb1,
            gf, gb, gp, r1, p2, r2, rb, z1, z2, zs, tt, to,
            s_tok, s_loc, s_g, s_dw, s_dx, s_vo, s_t, ss, rs):
     z = lax.axis_index('dp')
@@ -63,16 +63,20 @@
         return (pltpu.make_async_copy(xt.at[:, cols], xs.at[t], s_tok.at[0, t]),
                 pltpu.make_async_copy(dyt.at[:, cols], ys.at[t], s_tok.at[1, t]))
 
-    def gload(i, half):
-        r0 = pl.multiple_of(half * (6 * RT) + i * RT, RT)
-        return pltpu.make_async_copy(g.at[pl.ds(r0, RT), :], gf.at[i], s_g.at[i])
+    def gload(n):
+        own_half = n >= 6
+        o = n - 6
+        i = jnp.where(own_half, (o % 2) * 3 + o // 2, n)
+        h = jnp.where(own_half, k, 1 - k)
+        r0 = pl.multiple_of(h * (6 * RT) + i * RT, RT)
+        return pltpu.make_async_copy(g.at[pl.ds(r0, RT), :], gf.at[n % 4], s_g.at[n % 4])
 
     shards = ((w1, w3, w2), (v1, v3, v2))
     myrows = pl.ds(pl.multiple_of(k * SH, SH), SH)
     local_shards = [pltpu.make_async_copy(shards[u][m], pair.at[u, m, myrows, :], s_loc.at[3 * u + m])
                     for u in range(2) for m in range(3)]
-    for i in range(6):
-        gload(i, 1 - k).start()
+    for n in range(4):
+        gload(n).start()
     for c in local_shards:
         c.start()
 
@@ -95,17 +99,17 @@
     zo = z % 2
     qm = pl.ds(pl.multiple_of(k * HR + zo * QR, QR), QR)
     qo = pl.ds(pl.multiple_of(k * HR + (1 - zo) * QR, QR), QR)
-    w_x = rcopy(6, blk.at[0, :, qm, :], blk.at[1, :, qm, :], xn)
-    w_y = rcopy(7, blk.at[0, :, qm, :], blk.at[2, :, qm, :], yn)
-    w_zx = rcopy(8, blk.at[1, :, qm, :], blk.at[1, :, qm, :], zp)
-    w_zy = rcopy(9, blk.at[2, :, qm, :], blk.at[2, :, qm, :], zp)
-    w_f1a = rcopy(62, blk.at[1, :, qm, :], blk.at[1, :, qm, :], partner)
-    w_f1b = rcopy(63, blk.at[1, :, qo, :], blk.at[1, :, qo, :], partner)
-    w_f2a = rcopy(64, blk.at[2, :, qm, :], blk.at[2, :, qm, :], partner)
-    w_f2b = rcopy(65, blk.at[2, :, qo, :], blk.at[2, :, qo, :], partner)
-    w_da = rcopy(10, blk.at[1, :, qa, :], blk.at[3, :, qa, :], yn)
-    w_db = rcopy(11, blk.at[2, :, qb, :], blk.at[3, :, qb, :], xn)
-    w_f3 = rcopy(12, blk.at[3, :, half, :], blk.at[3, :, half, :], partner)
+    w_x = rcopy(6, blk.at[0, qm, :], blk.at[1, qm, :], xn)
+    w_y = rcopy(7, blk.at[0, qm, :], blk.at[2, qm, :], yn)
+    w_zx = rcopy(8, blk.at[1, qm, :], blk.at[1, qm, :], zp)
+    w_zy = rcopy(9, blk.at[2, qm, :], blk.at[2, qm, :], zp)
+    w_f1a = rcopy(62, blk.at[1, qm, :], blk.at[1, qm, :], partner)
+    w_f1b = rcopy(63, blk.at[1, qo, :], blk.at[1, qo, :], partner)
+    w_f2a = rcopy(64, blk.at[2, qm, :], blk.at[2, qm, :], partner)
+    w_f2b = rcopy(65, blk.at[2, qo, :], blk.at[2, qo, :], partner)
+    w_da = rcopy(10, blk.at[1, qa, :], blk.at[3, qa, :], yn)
+    w_db = rcopy(11, blk.at[2, qb, :], blk.at[3, qb, :], xn)
+    w_f3 = rcopy(12, blk.at[3, half, :], blk.at[3, half, :], partner)
 
     v_own = pltpu.make_async_copy(vblk, vo.at[:, :, blkcols(0, 0)], s_vo)
     def v_copies(m):
@@ -153,11 +157,11 @@
             c.start()
 
     def send_half(i, _):
-        gload(i, 1 - k).wait()
+        gload(i).wait()
         for q in range(4):
-            gb[i, q] = gf[i, :, q * FC:(q + 1) * FC].astype(jnp.bfloat16)
+            gb[i, q] = gf[i % 4, :, q * FC:(q + 1) * FC].astype(jnp.bfloat16)
         to_partner(i).start()
-        gload(i, k).start()
+        gload(i + 4).start()
         return 0
 
     lax.fori_loop(0, 6, send_half, 0)
@@ -165,20 +169,23 @@
     for m in range(3):
         local_shards[m].wait()
         to_pair[m].wait_recv()
-        blk[0, m] = pair[0, m].T
+        blk[0, :, m * FC:(m + 1) * FC] = pair[0, m].T
     w_x.start()
     w_y.start()
 
-    def own_tile(i):
-        gload(i, k).wait()
+    def own_tile(n, i):
+        gload(n).wait()
         to_partner(i).wait_recv()
         for q in range(4):
             gp[i, q] = (gp[i, q].astype(jnp.float32)
-                        + gf[i, :, q * FC:(q + 1) * FC].astype(jnp.bfloat16).astype(jnp.float32)).astype(jnp.bfloat16)
+                        + gf[n % 4, :, q * FC:(q + 1) * FC].astype(jnp.bfloat16).astype(jnp.float32)
+                        ).astype(jnp.bfloat16)
+        if n + 4 < 12:
+            gload(n + 4).start()
 
     def stage_a(j):
-        own_tile(j)
-        own_tile(3 + j)
+        own_tile(6 + 2 * j, j)
+        own_tile(7 + 2 * j, 3 + j)
         for b in range(2):
             first_x(j, b).start()
             first_y(j, b).start()
@@ -276,18 +283,22 @@
     }
     order = ('W1', 'WZ', 'W3', 'B', 'A', 'C', 'D0', 'D1', 'E0', 'E1', 'WD', 'V', 'V1')
 
-    def tick(step):
+    def tick(step, steps):
         for name in order:
             for j, n in enumerate(STEPS[name]):
-                if n < 24:
-                    pl.when(step == n)(functools.partial(stages[name], j))
+                if n in steps:
+                    if len(steps) == 1:
+                        stages[name](j)
+                    else:
+                        pl.when(step == n)(functools.partial(stages[name], j))
 
     def dw_out(c):
         cx, cy = c % 2, c // 2
         q = 2 * (y + cy - 2 * y * cy) + x + cx - 2 * x * cx
-        return pltpu.make_async_copy(dwa, dw.at[:, :, pl.ds(pl.multiple_of(q * FC, FC), FC)], s_dw)
-
-    def chunk(c, _):
+        return pltpu.make_async_copy(
+            dwa.at[c % 2], dw.at[:, :, pl.ds(pl.multiple_of(q * FC, FC), FC)], s_dw.at[c % 2])
+
+    def head(c):
         @pl.when(c == 1)
         def _():
             w_zx.wait_recv()
@@ -305,56 +316,80 @@
             w_f3.wait_recv()
 
         for m in range(3):
-            wt[m * FC:(m + 1) * FC, :] = blk[c, m].T
-
-        @pl.when(c > 0)
-        def _():
-            dw_out(c - 1).wait()
-
-        dwa[...] = jnp.zeros_like(dwa)
-
-        def tile(t, _):
-            step = c * NT + t
-
+            wt[m * FC:(m + 1) * FC, :] = blk[c, :, m * FC:(m + 1) * FC].T
+
+        @pl.when(c >= 2)
+        def _():
+            dw_out(c - 2).wait()
+
+        dwa[c % 2] = jnp.zeros((3, D, FC), jnp.float32)
+
+    def first_touch(t):
+        for cp in tok(t):
+            cp.wait()
+        dxa[t] = jnp.zeros((D, T), jnp.float32)
+
+    def forward(t, dab, hb):
+        xv = xs[t]
+        a = dot(wt[0:FC, :], xv)
+        b = dot(wt[FC:2 * FC, :], xv)
+        dh = dot(wt[2 * FC:3 * FC, :], ys[t])
+        sg = jnp.tanh(a * 0.5) * 0.5 + 0.5
+        act = a * sg
+        hb[...] = (act * b).astype(jnp.bfloat16)
+        dab[FC:, :] = (dh * act).astype(jnp.bfloat16)
+        dab[:FC, :] = (dh * b * (sg + act * (1.0 - sg))).astype(jnp.bfloat16)
+
+    def backward(step, dab, hb):
+        c, t = step // NT, step % NT
+        dxa[t] += dot(blk[c, :, :2 * FC], dab[...])
+        gw = dot(xs[t], dab[...], NTD)
+        dwa[c % 2, 0] += gw[:, :FC]
+        dwa[c % 2, 1] += gw[:, FC:]
+        dwa[c % 2, 2] += dot(ys[t], hb[...], NTD)
+
+    def half_step(step, steps, src, dst):
+        c, t = step // NT, step % NT
+        if any(n % NT == 0 for n in steps):
+            @pl.when(t == 0)
+            def _():
+                head(c)
+
+        if any(n % NT == 1 and n > NT for n in steps):
+            @pl.when((t == 1) & (c > 0))
+            def _():
+                dw_out(c - 1).start()
+
+        if any(n < NT for n in steps):
             @pl.when(c == 0)
             def _():
-                for cp in tok(t):
-                    cp.wait()
-                dxa[t] = jnp.zeros((D, T), jnp.float32)
-
-            tick(step)
-            xv = xs[t]
-            yv = ys[t]
-            a = dot(wt[0:FC, :], xv)
-            b = dot(wt[FC:2 * FC, :], xv)
-            dh = dot(wt[2 * FC:3 * FC, :], yv)
-            sg = jnp.tanh(a * 0.5) * 0.5 + 0.5
-            act = a * sg
-            hb[...] = (act * b).astype(jnp.bfloat16)
-            dab[FC:, :] = (dh * act).astype(jnp.bfloat16)
-            dab[:FC, :] = (dh * b * (sg + act * (1.0 - sg))).astype(jnp.bfloat16)
-            dxa[t] += dot(blk[c, 0], dab[:FC, :]) + dot(blk[c, 1], dab[FC:, :])
-            gw = dot(xv, dab[...], NTD)
-            dwa[0] += gw[:, :FC]
-            dwa[1] += gw[:, FC:]
-            dwa[2] += dot(yv, hb[...], NTD)
-            return 0
-
-        lax.fori_loop(0, NT, tile, 0)
-        dw_out(c).start()
+                first_touch(t)
+
+        tick(step, steps)
+        forward(t, *dst)
+        backward(step - 1, *src)
+
+    b0, b1 = (dab0, hb0), (dab1, hb1)
+    head(0)
+    first_touch(0)
+    tick(0, (0,))
+    forward(0, *b0)
+
+    def two_steps(p, _):
+        half_step(2 * p + 1, tuple(range(1, 23, 2)), b0, b1)
+        half_step(2 * p + 2, tuple(range(2, 23, 2)), b1, b0)
         return 0
 
-    lax.fori_loop(0, 4, chunk, 0)
+    lax.fori_loop(0, 11, two_steps, 0)
+    half_step(23, (23,), b0, b1)
+    backward(23, *b1)
+    dw_out(3).start()
 
     def dx_out(t):
-        return pltpu.make_async_copy(dxs.at[t % 2], dxt.at[:, pl.ds(pl.multiple_of(t * T, T), T)], s_dx.at[t % 2])
+        return pltpu.make_async_copy(xs.at[t], dxt.at[:, pl.ds(pl.multiple_of(t * T, T), T)], s_dx.at[t])
 
     def write_dx(t, _):
-        @pl.when(t >= 2)
-        def _():
-            dx_out(t - 2).wait()
-
-        dxs[t % 2] = dxa[t].astype(jnp.bfloat16)
+        xs[t] = dxa[t].astype(jnp.bfloat16)
         dx_out(t).start()
         return 0
 
@@ -376,15 +411,25 @@
         t_pair(i).wait_recv()
 
     def t_out(m):
-        return pltpu.make_async_copy(to.at[m, pl.ds(pl.multiple_of(k * SH, SH), SH), :], gs.at[m], s_t.at[m])
+        return pltpu.make_async_copy(to.at[m], gs.at[m], s_t.at[m])
 
     for m in range(3):
-        to[m] = jnp.concatenate([tt[(4 * m + r) // 6, (4 * m + r) % 6] for r in range(4)], axis=0).T
+        full = jnp.concatenate([tt[(4 * m + r) // 6, (4 * m + r) % 6] for r in range(4)], axis=0).T
+
+        @pl.when(k == 0)
+        def _():
+            to[m] = full[:SH]
+
+        @pl.when(k == 1)
+        def _():
+            to[m] = full[SH:]
+
         t_out(m).start()
 
+    dw_out(2).wait()
     dw_out(3).wait()
-    dx_out(NT - 2).wait()
-    dx_out(NT - 1).wait()
+    for t in range(NT):
+        dx_out(t).wait()
     v_own.wait()
     for m in range(3):
         t_out(m).wait()
@@ -430,13 +475,13 @@
         in_specs=[any_spec] * 9,
         out_specs=(any_spec,) * 4,
         scratch_shapes=[
-            V((NT, D, T), bf), V((NT, D, T), bf), V((2, 3, FC, D), bf), V((4, 3, D, FC), bf), V((3, D, FC), bf),
-            V((3 * FC, D), bf), V((NT, D, T), f32), V((3, D, FC), f32), V((2 * FC, T), bf), V((FC, T), bf),
-            V((2, D, T), bf),
-            V((6, RT, F), f32), V((6, 4, RT, FC), bf), V((6, 4, RT, FC), bf), V((6, 2, RT, FC), bf),
+            V((NT, D, T), bf), V((NT, D, T), bf), V((2, 3, FC, D), bf), V((4, D, 3 * FC), bf), V((3, D, FC), bf),
+            V((3 * FC, D), bf), V((NT, D, T), f32), V((2, 3, D, FC), f32),
+            V((2 * FC, T), bf), V((FC, T), bf), V((2 * FC, T), bf), V((FC, T), bf),
+            V((4, RT, F), f32), V((6, 4, RT, FC), bf), V((6, 4, RT, FC), bf), V((6, 2, RT, FC), bf),
             V((6, 2, RT, FC), bf), V((6, RT, FC), bf), V((6, RT, FC), bf), V((6, RT, FC), bf),
-            V((6, RT, FC), f32), V((6, RT, FC), f32), V((2, 6, RT, FC), f32), V((3, FC, D), f32),
-            dma((2, NT)), dma((6,)), dma((6,)), dma, dma((2,)), dma, dma((3,)), dma((93,)), dma((93,)),
+            V((6, RT, FC), f32), V((6, RT, FC), f32), V((2, 6, RT, FC), f32), V((3, SH, D), f32),
+            dma((2, NT)), dma((6,)), dma((4,)), dma((2,)), dma((NT,)), dma, dma((3,)), dma((93,)), dma((93,)),
         ],
         compiler_params=pltpu.CompilerParams(
             collective_id=0, has_side_effects=True, vmem_limit_bytes=67_000_000),

time: 121 us -> 108 us (0.89)
  Pallas kernels: 104 us -> 91.3 us
    pallas_call x1, Pallas kernels: 104 us -> 91.3 us  [step_kernel(): pl.pallas_call(kernel, name='mlp_step', out_shape=(jax.ShapeDtypeStruct((...]
where the time goes in v3:
time: 108 us; the launch traced here: 107 us
  Pallas kernels  91.3 us (85%)
  local copies, waits for them, and re-layouts  15.5 us (14%)
    pallas_call x1, Pallas kernels, step_kernel(): pl.pallas_call(kernel, name='mlp_step', out_shape=(jax.ShapeDtypeStruct((...  91.3 us
    unnamed x11, local copies, waits for them, and re-layouts  10 us
    transpose x1, local copies, waits for them, and re-layouts, device_step(): return (dxt.T, gs.transpose(0, 2, 1), dw[None], vo[0], vo[1], vo[2].T)  5.5 us

profile of v3, /device:TPU:0, one launch (start us, length us, event | category | flops | bytes accessed | tf_op | source)
XLA Modules:
  0.0 107.5 jit_solution(10088338292828529131)
XLA Ops:
  0.6 91.3 %mlp_step.1 = (bf16[576,3072]{1,0:T(8,128)(2,1)}, f32[3,576,1536]{2,1,0:T(8,128)}, bf16[3,576,1536]{2,1,0:T(8,128)(2,1)}, f32[3,192,576]{2,1,0:T(8,128)}) custom-call(bf16[576,3072]{1,0:T(8,128)(2,1)} %bitcast.24, bf16[576,3072]{1,0:T(8,128)(2,1)} %bitcast.25, bf16[192,576]{1,0:T(8,128)(2,1)} %bitcast.26, bf16[192,576]{1,0:T(8,128)(2,1)} %bitcast.27, ...), custom_call_target="tpu_custom_call" | custom-call | flops 43499999232 | bytes 60000000 | tf_op jit(solution)/shard_map/mlp_step/pallas_call | solution.py:470
  91.9 0.0 slice-start
  91.9 0.0 slice-start.1
  92.0 5.5 %slice_bitcast_fusion = (bf16[1536,576]{0,1:T(8,128)(2,1)}, bf16[576,1536]{1,0:T(8,128)(2,1)}, bf16[576,1536]{1,0:T(8,128)(2,1)}) fusion(bf16[3,576,1536]{2,1,0:T(8,128)(2,1)} %get-tuple-element.13), kind=kLoop, calls=%fused_computation | loop fusion | bytes 10616832 | tf_op jit(solution)/shard_map/transpose | solution.py:496
  97.5 0.0 copy-start
  97.5 0.0 slice-start.2
  97.5 4.7 %copy.18 = bf16[3072,576]{0,1:T(8,128)(2,1)} copy(bf16[3072,576]{0,1:T(8,128)(2,1)} %bitcast.21) | data formatting | bytes 7077888
  102.2 0.0 copy-done
  102.2 1.1 %copy.19 = f32[3,576,192]{1,2,0:T(8,128)} copy(f32[3,576,192]{1,2,0:T(8,128)S(1)} %bitcast.22) | data formatting | bytes 2654208
  103.3 0.0 slice-done
  103.3 0.0 slice-done.1
  103.3 0.0 slice-done.2
  103.3 4.1 %copy.20 = f32[1,3,576,1536]{3,2,1,0:T(8,128)} copy(f32[1,3,576,1536]{3,2,1,0:T(8,128)S(1)} %bitcast.20) | data formatting | bytes 21233664
  (1 shorter events, 0.0 us)
Async XLA Ops:
  91.9 11.4 %slice-start = ((s8[10616832]{0:T(1024)(128)(4,1)}), s8[4194304]{0:T(1024)(128)(4,1)S(1)}, s32[]{:S(2)}) async-start(s8[10616832]{0:T(1024)(128)(4,1)} %bitcast.18), calls=%async_computation | async-start | bytes 8388608
  91.9 11.4 %slice-start.1 = ((s8[10616832]{0:T(1024)(128)(4,1)}), s8[4194304]{0:T(1024)(128)(4,1)S(1)}, s32[]{:S(2)}) async-start(s8[10616832]{0:T(1024)(128)(4,1)} %bitcast.18), calls=%async_computation.1 | async-start | bytes 8388608
  97.5 4.8 %copy-start = (f32[3,192,576]{2,1,0:T(8,128)S(1)}, f32[3,192,576]{2,1,0:T(8,128)}, u32[]{:S(2)}) copy-start(f32[3,192,576]{2,1,0:T(8,128)} %get-tuple-element.11) | copy-start | bytes 3981316
  97.5 5.9 %slice-start.2 = ((s8[10616832]{0:T(1024)(128)(4,1)}), s8[2228224]{0:T(1024)(128)(4,1)S(1)}, s32[]{:S(2)}) async-start(s8[10616832]{0:T(1024)(128)(4,1)} %bitcast.18), calls=%async_computation.2 | async-start | bytes 4456448

commit v4 on v3

--- a/solution.py
+++ b/solution.py
@@ -25,9 +25,9 @@
 NTD = (((1,), (1,)), ((), ()))
 
 STEPS = {
-    'A': (0, 1, 6), 'W1': (4,), 'WZ': (9,), 'WD': (12,), 'W3': (16,), 'V': (13,), 'V1': (20, 22, 24),
-    'B': (6, 7, 10), 'C': (8, 11, 12),
-    'D0': (10, 14, 17), 'D1': (12, 16, 19), 'E0': (14, 18, 22), 'E1': (16, 20, 24),
+    'AX': (0, 5, 7), 'AY': (0, 1, 2), 'BX': (7, 10, 13), 'BY': (5, 6, 8), 'CX': (9, 13, 15), 'CY': (8, 11, 14),
+    'W1': (3,), 'WZ': (6,), 'WDA': (7,), 'WDB': (9,), 'W3': (16,), 'V': (13,), 'V1': (18, 20, 22),
+    'D0': (11, 15, 17), 'D1': (10, 13, 16), 'E0': (15, 19, 22), 'E1': (13, 17, 20),
 }
 
 
@@ -63,10 +63,13 @@
         return (pltpu.make_async_copy(xt.at[:, cols], xs.at[t], s_tok.at[0, t]),
                 pltpu.make_async_copy(dyt.at[:, cols], ys.at[t], s_tok.at[1, t]))
 
+    def g_tile(o):
+        return jnp.where(o == 0, 0, jnp.where(o < 4, o + 2, o - 3))
+
     def gload(n):
         own_half = n >= 6
-        o = n - 6
-        i = jnp.where(own_half, (o % 2) * 3 + o // 2, n)
+        o = jnp.where(own_half, n - 6, n)
+        i = g_tile(o)
         h = jnp.where(own_half, k, 1 - k)
         r0 = pl.multiple_of(h * (6 * RT) + i * RT, RT)
         return pltpu.make_async_copy(g.at[pl.ds(r0, RT), :], gf.at[n % 4], s_g.at[n % 4])
@@ -99,12 +102,10 @@
     zo = z % 2
     qm = pl.ds(pl.multiple_of(k * HR + zo * QR, QR), QR)
     qo = pl.ds(pl.multiple_of(k * HR + (1 - zo) * QR, QR), QR)
-    w_x = rcopy(6, blk.at[0, qm, :], blk.at[1, qm, :], xn)
+    w_x = rcopy(6, blk.at[0, half, :], blk.at[1, half, :], xn)
     w_y = rcopy(7, blk.at[0, qm, :], blk.at[2, qm, :], yn)
-    w_zx = rcopy(8, blk.at[1, qm, :], blk.at[1, qm, :], zp)
     w_zy = rcopy(9, blk.at[2, qm, :], blk.at[2, qm, :], zp)
-    w_f1a = rcopy(62, blk.at[1, qm, :], blk.at[1, qm, :], partner)
-    w_f1b = rcopy(63, blk.at[1, qo, :], blk.at[1, qo, :], partner)
+    w_f1 = rcopy(62, blk.at[1, half, :], blk.at[1, half, :], partner)
     w_f2a = rcopy(64, blk.at[2, qm, :], blk.at[2, qm, :], partner)
     w_f2b = rcopy(65, blk.at[2, qo, :], blk.at[2, qo, :], partner)
     w_da = rcopy(10, blk.at[1, qa, :], blk.at[3, qa, :], yn)
@@ -156,15 +157,16 @@
         for c in tok(t):
             c.start()
 
-    def send_half(i, _):
-        gload(i).wait()
+    def send_half(n, _):
+        i = g_tile(n)
+        gload(n).wait()
         for q in range(4):
-            gb[i, q] = gf[i % 4, :, q * FC:(q + 1) * FC].astype(jnp.bfloat16)
+            gb[i, q] = gf[n % 4, :, q * FC:(q + 1) * FC].astype(jnp.bfloat16)
         to_partner(i).start()
-        gload(i + 4).start()
+        gload(n + 4).start()
         return 0
 
-    lax.fori_loop(0, 6, send_half, 0)
+    lax.fori_loop(0, 2, send_half, 0)
 
     for m in range(3):
         local_shards[m].wait()
@@ -172,8 +174,10 @@
         blk[0, :, m * FC:(m + 1) * FC] = pair[0, m].T
     w_x.start()
     w_y.start()
-
-    def own_tile(n, i):
+    lax.fori_loop(2, 6, send_half, 0)
+
+    def own_tile(i):
+        n = 6 + (0, 4, 5, 1, 2, 3)[i]
         gload(n).wait()
         to_partner(i).wait_recv()
         for q in range(4):
@@ -183,21 +187,27 @@
         if n + 4 < 12:
             gload(n + 4).start()
 
-    def stage_a(j):
-        own_tile(6 + 2 * j, j)
-        own_tile(7 + 2 * j, 3 + j)
+    def stage_ax(j):
+        own_tile(j)
         for b in range(2):
             first_x(j, b).start()
+
+    def stage_ay(j):
+        own_tile(3 + j)
+        for b in range(2):
             first_y(j, b).start()
 
-    def stage_b(j):
+    def stage_bx(j):
         for b in range(2):
             first_x(j, b).wait_recv()
             p2[j, b] = (gp[j, 2 * b + x].astype(jnp.float32) + r1[j, b].astype(jnp.float32)).astype(jnp.bfloat16)
+        second_y(j).start()
+
+    def stage_by(j):
+        for b in range(2):
             first_y(j, b).wait_recv()
             p2[3 + j, b] = (gp[3 + j, 2 * y + b].astype(jnp.float32)
                             + r1[3 + j, b].astype(jnp.float32)).astype(jnp.bfloat16)
-        second_y(j).start()
         second_x(j).start()
 
     def second(i):
@@ -206,13 +216,12 @@
     def mine(i):
         return y if i < 3 else x
 
-    def stage_c(j):
+    def stage_c(i):
         @pl.when(at_end)
         def _():
-            for i in (j, 3 + j):
-                second(i).wait_recv()
-                rb[i] = (p2[i, mine(i)].astype(jnp.float32) + r2[i].astype(jnp.float32)).astype(jnp.bfloat16)
-                z_in(i).start()
+            second(i).wait_recv()
+            rb[i] = (p2[i, mine(i)].astype(jnp.float32) + r2[i].astype(jnp.float32)).astype(jnp.bfloat16)
+            z_in(i).start()
 
     def stage_d(i):
         @pl.when(inner)
@@ -240,9 +249,6 @@
         v_own.start()
 
     def w_1():
-        w_x.wait_recv()
-        w_zx.start()
-        w_f1a.start()
         w_y.wait_recv()
         w_zy.start()
         w_f2a.start()
@@ -250,10 +256,6 @@
     def w_z():
         w_zy.wait_recv()
         w_f2b.start()
-
-    def w_d():
-        w_da.start()
-        w_db.start()
 
     def w_3():
         w_da.wait_recv()
@@ -276,12 +278,14 @@
         v_f3.start()
 
     stages = {
-        'A': stage_a, 'B': stage_b, 'C': stage_c,
+        'AX': stage_ax, 'AY': stage_ay, 'BX': stage_bx, 'BY': stage_by,
+        'CX': stage_c, 'CY': lambda j: stage_c(3 + j),
         'D0': stage_d, 'D1': lambda j: stage_d(3 + j), 'E0': stage_e, 'E1': lambda j: stage_e(3 + j),
         'V': lambda j: v_start(), 'V1': v_1,
-        'W1': lambda j: w_1(), 'WZ': lambda j: w_z(), 'WD': lambda j: w_d(), 'W3': lambda j: w_3(),
+        'W1': lambda j: w_1(), 'WZ': lambda j: w_z(), 'WDA': lambda j: w_da.start(), 'WDB': lambda j: w_db.start(),
+        'W3': lambda j: w_3(),
     }
-    order = ('W1', 'WZ', 'W3', 'B', 'A', 'C', 'D0', 'D1', 'E0', 'E1', 'WD', 'V', 'V1')
+    order = ('W1', 'WZ', 'W3', 'BX', 'BY', 'AX', 'AY', 'CX', 'CY', 'D0', 'D1', 'E0', 'E1', 'WDA', 'WDB', 'V', 'V1')
 
     def tick(step, steps):
         for name in order:
@@ -301,10 +305,9 @@
     def head(c):
         @pl.when(c == 1)
         def _():
-            w_zx.wait_recv()
-            w_f1b.start()
-            w_f1a.wait_recv()
-            w_f1b.wait_recv()
+            w_x.wait_recv()
+            w_f1.start()
+            w_f1.wait_recv()
 
         @pl.when(c == 2)
         def _():
@@ -453,7 +456,7 @@
         second_y(j).wait_send()
     for c in to_pair:
         c.wait_send()
-    for c in (w_x, w_y, w_zx, w_zy, w_f1a, w_f1b, w_f2a, w_f2b, w_da, w_db, w_f3):
+    for c in (w_x, w_y, w_zy, w_f1, w_f2a, w_f2b, w_da, w_db, w_f3):
         c.wait_send()
     for m in range(3):
         for c in v_copies(m):

time: 108 us -> 99.3 us (0.919)
  Pallas kernels: 91.3 us -> 82.8 us
    pallas_call x1, Pallas kernels: 91.3 us -> 82.8 us  [step_kernel(): pl.pallas_call(kernel, name='mlp_step', out_shape=(jax.ShapeDtypeStruct((...]
where the time goes in v4:
time: 99.3 us; the launch traced here: 99 us
  Pallas kernels  82.8 us (83%)
  local copies, waits for them, and re-layouts  15.5 us (16%)
    pallas_call x1, Pallas kernels, step_kernel(): pl.pallas_call(kernel, name='mlp_step', out_shape=(jax.ShapeDtypeStruct((...  82.8 us
    unnamed x11, local copies, waits for them, and re-layouts  10 us
    transpose x1, local copies, waits for them, and re-layouts, device_step(): return (dxt.T, gs.transpose(0, 2, 1), dw[None], vo[0], vo[1], vo[2].T)  5.5 us

profile of v4, /device:TPU:0, one launch (start us, length us, event | category | flops | bytes accessed | tf_op | source)
XLA Modules:
  0.0 99.0 jit_solution(6094736314569399611)
XLA Ops:
  0.6 82.8 %mlp_step.1 = (bf16[576,3072]{1,0:T(8,128)(2,1)}, f32[3,576,1536]{2,1,0:T(8,128)}, bf16[3,576,1536]{2,1,0:T(8,128)(2,1)}, f32[3,192,576]{2,1,0:T(8,128)}) custom-call(bf16[576,3072]{1,0:T(8,128)(2,1)} %bitcast.24, bf16[576,3072]{1,0:T(8,128)(2,1)} %bitcast.25, bf16[192,576]{1,0:T(8,128)(2,1)} %bitcast.26, bf16[192,576]{1,0:T(8,128)(2,1)} %bitcast.27, ...), custom_call_target="tpu_custom_call" | custom-call | flops 43499999232 | bytes 60000000 | tf_op jit(solution)/shard_map/mlp_step/pallas_call | solution.py:473
  83.5 0.0 slice-start
  83.5 0.0 slice-start.1
  83.5 5.5 %slice_bitcast_fusion = (bf16[1536,576]{0,1:T(8,128)(2,1)}, bf16[576,1536]{1,0:T(8,128)(2,1)}, bf16[576,1536]{1,0:T(8,128)(2,1)}) fusion(bf16[3,576,1536]{2,1,0:T(8,128)(2,1)} %get-tuple-element.13), kind=kLoop, calls=%fused_computation | loop fusion | bytes 10616832 | tf_op jit(solution)/shard_map/transpose | solution.py:499
  89.0 0.0 copy-start
  89.0 0.0 slice-start.2
  89.0 4.7 %copy.18 = bf16[3072,576]{0,1:T(8,128)(2,1)} copy(bf16[3072,576]{0,1:T(8,128)(2,1)} %bitcast.21) | data formatting | bytes 7077888
  93.8 0.0 copy-done
  93.8 1.1 %copy.19 = f32[3,576,192]{1,2,0:T(8,128)} copy(f32[3,576,192]{1,2,0:T(8,128)S(1)} %bitcast.22) | data formatting | bytes 2654208
  94.9 0.0 slice-done
  94.9 0.0 slice-done.1
  94.9 0.0 slice-done.2
  94.9 4.1 %copy.20 = f32[1,3,576,1536]{3,2,1,0:T(8,128)} copy(f32[1,3,576,1536]{3,2,1,0:T(8,128)S(1)} %bitcast.20) | data formatting | bytes 21233664
  (1 shorter events, 0.0 us)
Async XLA Ops:
  83.5 11.4 %slice-start = ((s8[10616832]{0:T(1024)(128)(4,1)}), s8[4194304]{0:T(1024)(128)(4,1)S(1)}, s32[]{:S(2)}) async-start(s8[10616832]{0:T(1024)(128)(4,1)} %bitcast.18), calls=%async_computation | async-start | bytes 8388608
  83.5 11.4 %slice-start.1 = ((s8[10616832]{0:T(1024)(128)(4,1)}), s8[4194304]{0:T(1024)(128)(4,1)S(1)}, s32[]{:S(2)}) async-start(s8[10616832]{0:T(1024)(128)(4,1)} %bitcast.18), calls=%async_computation.1 | async-start | bytes 8388608
  89.0 4.8 %copy-start = (f32[3,192,576]{2,1,0:T(8,128)S(1)}, f32[3,192,576]{2,1,0:T(8,128)}, u32[]{:S(2)}) copy-start(f32[3,192,576]{2,1,0:T(8,128)} %get-tuple-element.11) | copy-start | bytes 3981316
  89.0 5.9 %slice-start.2 = ((s8[10616832]{0:T(1024)(128)(4,1)}), s8[2228224]{0:T(1024)(128)(4,1)S(1)}, s32[]{:S(2)}) async-start(s8[10616832]{0:T(1024)(128)(4,1)} %bitcast.18), calls=%async_computation.2 | async-start | bytes 4456448

commit v5 on v4

--- a/solution.py
+++ b/solution.py
@@ -36,9 +36,10 @@
 
 
 def kernel(xt, dyt, w1, w3, w2, v1, v3, v2, g, dxt, dw, vo, gs,
-           xs, ys, pair, blk, vblk, wt, dxa, dwa, dab0, hb0, dab1, hb1,
-           gf, gb, gp, r1, p2, r2, rb, z1, z2, zs, tt, to,
-           s_tok, s_loc, s_g, s_dw, s_dx, s_vo, s_t, ss, rs):
+           ys, pair, blk, vblk, wt, dxa, dab0, hb0, dab1, hb1,
+           gf, gb, gp, r1, r2, zb, z2, zs, tp,
+           s_tok, s_loc, s_g, s_vo, ss, rs):
+    xs = dxt
     z = lax.axis_index('dp')
     y = lax.axis_index('col')
     f = lax.axis_index('fsdp')
@@ -60,7 +61,7 @@
 
     def tok(t):
         cols = pl.ds(pl.multiple_of(t * T, T), T)
-        return (pltpu.make_async_copy(xt.at[:, cols], xs.at[t], s_tok.at[0, t]),
+        return (pltpu.make_async_copy(xt.at[:, cols], xs.at[:, cols], s_tok.at[0, t]),
                 pltpu.make_async_copy(dyt.at[:, cols], ys.at[t], s_tok.at[1, t]))
 
     def g_tile(o):
@@ -134,22 +135,22 @@
         return rcopy(32 + 2 * j + xx, gp.at[3 + j, 2 * (1 - y) + xx], r1.at[3 + j, xx], yn)
 
     def second_y(j):
-        return rcopy(38 + j, p2.at[j, 1 - y], r2.at[j], yn)
+        return rcopy(38 + j, r1.at[j, 1 - y], r2.at[j], yn)
 
     def second_x(j):
-        return rcopy(41 + j, p2.at[3 + j, 1 - x], r2.at[3 + j], xn)
+        return rcopy(41 + j, r1.at[3 + j, 1 - x], r2.at[3 + j], xn)
 
     def z_in(i):
-        return rcopy(44 + i, rb.at[i], z1.at[i], zp)
+        return rcopy(44 + i, zb.at[i], zb.at[i], zp)
 
     def z_mid(i):
         return rcopy(50 + i, zs.at[i], z2.at[i], zm)
 
     def z_out(i):
-        return rcopy(56 + i, tt.at[k, i], tt.at[k, i], zp)
+        return rcopy(56 + i, z2.at[i], z2.at[i], zp)
 
     def t_pair(i):
-        return rcopy(87 + i, tt.at[k, i], tt.at[k, i], partner)
+        return rcopy(87 + i, z2.at[i], tp.at[i], partner)
 
     for c in to_pair:
         c.start()
@@ -200,13 +201,13 @@
     def stage_bx(j):
         for b in range(2):
             first_x(j, b).wait_recv()
-            p2[j, b] = (gp[j, 2 * b + x].astype(jnp.float32) + r1[j, b].astype(jnp.float32)).astype(jnp.bfloat16)
+            r1[j, b] = (gp[j, 2 * b + x].astype(jnp.float32) + r1[j, b].astype(jnp.float32)).astype(jnp.bfloat16)
         second_y(j).start()
 
     def stage_by(j):
         for b in range(2):
             first_y(j, b).wait_recv()
-            p2[3 + j, b] = (gp[3 + j, 2 * y + b].astype(jnp.float32)
+            r1[3 + j, b] = (gp[3 + j, 2 * y + b].astype(jnp.float32)
                             + r1[3 + j, b].astype(jnp.float32)).astype(jnp.bfloat16)
         second_x(j).start()
 
@@ -220,7 +221,7 @@
         @pl.when(at_end)
         def _():
             second(i).wait_recv()
-            rb[i] = (p2[i, mine(i)].astype(jnp.float32) + r2[i].astype(jnp.float32)).astype(jnp.bfloat16)
+            zb[i] = (r1[i, mine(i)].astype(jnp.float32) + r2[i].astype(jnp.float32)).astype(jnp.bfloat16)
             z_in(i).start()
 
     def stage_d(i):
@@ -228,14 +229,14 @@
         def _():
             second(i).wait_recv()
             z_in(i).wait_recv()
-            zs[i] = (p2[i, mine(i)].astype(jnp.float32) + r2[i].astype(jnp.float32)) + z1[i].astype(jnp.float32)
+            zs[i] = (r1[i, mine(i)].astype(jnp.float32) + r2[i].astype(jnp.float32)) + zb[i].astype(jnp.float32)
             z_mid(i).start()
 
     def stage_e(i):
         @pl.when(inner)
         def _():
             z_mid(i).wait_recv()
-            tt[k, i] = zs[i] + z2[i]
+            z2[i] = zs[i] + z2[i]
             z_out(i).start()
             t_pair(i).start()
 
@@ -296,11 +297,10 @@
                     else:
                         pl.when(step == n)(functools.partial(stages[name], j))
 
-    def dw_out(c):
+    def dw_cols(c):
         cx, cy = c % 2, c // 2
         q = 2 * (y + cy - 2 * y * cy) + x + cx - 2 * x * cx
-        return pltpu.make_async_copy(
-            dwa.at[c % 2], dw.at[:, :, pl.ds(pl.multiple_of(q * FC, FC), FC)], s_dw.at[c % 2])
+        return pl.ds(pl.multiple_of(q * FC, FC), FC)
 
     def head(c):
         @pl.when(c == 1)
@@ -321,19 +321,18 @@
         for m in range(3):
             wt[m * FC:(m + 1) * FC, :] = blk[c, :, m * FC:(m + 1) * FC].T
 
-        @pl.when(c >= 2)
-        def _():
-            dw_out(c - 2).wait()
-
-        dwa[c % 2] = jnp.zeros((3, D, FC), jnp.float32)
+        dw[:, :, dw_cols(c)] = jnp.zeros((3, D, FC), jnp.float32)
 
     def first_touch(t):
         for cp in tok(t):
             cp.wait()
         dxa[t] = jnp.zeros((D, T), jnp.float32)
 
+    def tcols(t):
+        return pl.ds(pl.multiple_of(t * T, T), T)
+
     def forward(t, dab, hb):
-        xv = xs[t]
+        xv = xs[:, tcols(t)]
         a = dot(wt[0:FC, :], xv)
         b = dot(wt[FC:2 * FC, :], xv)
         dh = dot(wt[2 * FC:3 * FC, :], ys[t])
@@ -346,10 +345,11 @@
     def backward(step, dab, hb):
         c, t = step // NT, step % NT
         dxa[t] += dot(blk[c, :, :2 * FC], dab[...])
-        gw = dot(xs[t], dab[...], NTD)
-        dwa[c % 2, 0] += gw[:, :FC]
-        dwa[c % 2, 1] += gw[:, FC:]
-        dwa[c % 2, 2] += dot(ys[t], hb[...], NTD)
+        gw = dot(xs[:, tcols(t)], dab[...], NTD)
+        cols = dw_cols(c)
+        dw[0, :, cols] += gw[:, :FC]
+        dw[1, :, cols] += gw[:, FC:]
+        dw[2, :, cols] += dot(ys[t], hb[...], NTD)
 
     def half_step(step, steps, src, dst):
         c, t = step // NT, step % NT
@@ -358,11 +358,6 @@
             def _():
                 head(c)
 
-        if any(n % NT == 1 and n > NT for n in steps):
-            @pl.when((t == 1) & (c > 0))
-            def _():
-                dw_out(c - 1).start()
-
         if any(n < NT for n in steps):
             @pl.when(c == 0)
             def _():
@@ -386,14 +381,9 @@
     lax.fori_loop(0, 11, two_steps, 0)
     half_step(23, (23,), b0, b1)
     backward(23, *b1)
-    dw_out(3).start()
-
-    def dx_out(t):
-        return pltpu.make_async_copy(xs.at[t], dxt.at[:, pl.ds(pl.multiple_of(t * T, T), T)], s_dx.at[t])
 
     def write_dx(t, _):
-        xs[t] = dxa[t].astype(jnp.bfloat16)
-        dx_out(t).start()
+        xs[:, tcols(t)] = dxa[t].astype(jnp.bfloat16)
         return 0
 
     lax.fori_loop(0, NT, write_dx, 0)
@@ -413,29 +403,18 @@
     for i in range(6):
         t_pair(i).wait_recv()
 
-    def t_out(m):
-        return pltpu.make_async_copy(to.at[m], gs.at[m], s_t.at[m])
-
     for m in range(3):
-        full = jnp.concatenate([tt[(4 * m + r) // 6, (4 * m + r) % 6] for r in range(4)], axis=0).T
-
-        @pl.when(k == 0)
-        def _():
-            to[m] = full[:SH]
-
-        @pl.when(k == 1)
-        def _():
-            to[m] = full[SH:]
-
-        t_out(m).start()
-
-    dw_out(2).wait()
-    dw_out(3).wait()
-    for t in range(NT):
-        dx_out(t).wait()
+        for kk in range(2):
+            @pl.when(k == kk)
+            def _():
+                tiles = []
+                for r in range(4 * m, 4 * m + 4):
+                    src = z2 if r // 6 == kk else tp
+                    tiles.append(src[r % 6])
+                full = jnp.concatenate(tiles, axis=0).T
+                gs[m] = full[kk * SH:(kk + 1) * SH]
+
     v_own.wait()
-    for m in range(3):
-        t_out(m).wait()
     for i in range(6):
         t_pair(i).wait_send()
         to_partner(i).wait_send()
@@ -467,27 +446,26 @@
 
 def step_kernel(xt, dyt, w1, w3, w2, v1, v3, v2, g):
     any_spec = pl.BlockSpec(memory_space=pl.ANY)
+    vmem = pl.BlockSpec(memory_space=pltpu.VMEM)
     bf, f32 = jnp.bfloat16, jnp.float32
     V = pltpu.VMEM
     dma = pltpu.SemaphoreType.DMA
     return pl.pallas_call(
         kernel,
         name='mlp_step',
-        out_shape=(jax.ShapeDtypeStruct((D, N), bf), jax.ShapeDtypeStruct((3, D, F), f32),
-                   jax.ShapeDtypeStruct((3, D, F), bf), jax.ShapeDtypeStruct((3, SH, D), f32)),
+        out_shape=(V((D, N), bf), V((3, D, F), f32), jax.ShapeDtypeStruct((3, D, F), bf), V((3, SH, D), f32)),
         in_specs=[any_spec] * 9,
-        out_specs=(any_spec,) * 4,
+        out_specs=(vmem, vmem, any_spec, vmem),
         scratch_shapes=[
-            V((NT, D, T), bf), V((NT, D, T), bf), V((2, 3, FC, D), bf), V((4, D, 3 * FC), bf), V((3, D, FC), bf),
-            V((3 * FC, D), bf), V((NT, D, T), f32), V((2, 3, D, FC), f32),
+            V((NT, D, T), bf), V((2, 3, FC, D), bf), V((4, D, 3 * FC), bf), V((3, D, FC), bf),
+            V((3 * FC, D), bf), V((NT, D, T), f32),
             V((2 * FC, T), bf), V((FC, T), bf), V((2 * FC, T), bf), V((FC, T), bf),
             V((4, RT, F), f32), V((6, 4, RT, FC), bf), V((6, 4, RT, FC), bf), V((6, 2, RT, FC), bf),
-            V((6, 2, RT, FC), bf), V((6, RT, FC), bf), V((6, RT, FC), bf), V((6, RT, FC), bf),
-            V((6, RT, FC), f32), V((6, RT, FC), f32), V((2, 6, RT, FC), f32), V((3, SH, D), f32),
-            dma((2, NT)), dma((6,)), dma((4,)), dma((2,)), dma((NT,)), dma, dma((3,)), dma((93,)), dma((93,)),
+            V((6, RT, FC), bf), V((6, RT, FC), bf), V((6, RT, FC), f32), V((6, RT, FC), f32), V((6, RT, FC), f32),
+            dma((2, NT)), dma((6,)), dma((4,)), dma, dma((93,)), dma((93,)),
         ],
         compiler_params=pltpu.CompilerParams(
-            collective_id=0, has_side_effects=True, vmem_limit_bytes=67_000_000),
+            collective_id=0, has_side_effects=True, vmem_limit_bytes=50_800_000),
         cost_estimate=pl.CostEstimate(flops=43_500_000_000, bytes_accessed=60_000_000, transcendentals=4_718_592),
     )(xt, dyt, w1, w3, w2, v1, v3, v2, g)
 

time: 99.3 us -> 94.2 us (0.949)
  local copies, waits for them, and re-layouts: 15.5 us -> 10.9 us
    transpose x1, local copies, waits for them, and re-layouts: 5.5 us -> 2.48 us  [device_step(): return (dxt.T, gs.transpose(0, 2, 1), dw[None], vo[0], vo[1], vo[2].T)]
    unnamed x11 -> x7, local copies, waits for them, and re-layouts: 10 us -> 8.43 us
where the time goes in v5:
time: 94.2 us; the launch traced here: 94.1 us
  Pallas kernels  82.5 us (88%)
  local copies, waits for them, and re-layouts  10.9 us (12%)
    pallas_call x1, Pallas kernels, step_kernel(): pl.pallas_call(kernel, name='mlp_step', out_shape=(V((D, N), bf), V((3, D...  82.5 us
    unnamed x7, local copies, waits for them, and re-layouts  8.43 us
    transpose x1, local copies, waits for them, and re-layouts, device_step(): return (dxt.T, gs.transpose(0, 2, 1), dw[None], vo[0], vo[1], vo[2].T)  2.48 us

profile of v5, /device:TPU:0, one launch (start us, length us, event | category | flops | bytes accessed | tf_op | source)
XLA Modules:
  0.0 94.1 jit_solution(8194441544829424599)
XLA Ops:
  0.6 82.5 %mlp_step.1 = (bf16[576,3072]{1,0:T(8,128)(2,1)S(1)}, f32[3,576,1536]{2,1,0:T(8,128)S(1)}, bf16[3,576,1536]{2,1,0:T(8,128)(2,1)}, f32[3,192,576]{2,1,0:T(8,128)S(1)}) custom-call(bf16[576,3072]{1,0:T(8,128)(2,1)} %bitcast.24, bf16[576,3072]{1,0:T(8,128)(2,1)} %bitcast.25, bf16[192,576]{1,0:T(8,128)(2,1)} %bitcast.26, bf16[192,576]{1,0:T(8,128)(2,1)} %bitcast.27, ...), custom_call_target="tpu_custom_call" | custom-call | flops 43499999232 | bytes 60000000 | tf_op jit(solution)/shard_map/mlp_step/pallas_call | solution.py:453
  83.1 0.0 slice-start
  83.2 0.0 slice-start.1
  83.2 1.8 %copy.18 = bf16[3072,576]{0,1:T(8,128)(2,1)} copy(bf16[3072,576]{0,1:T(8,128)(2,1)S(1)} %bitcast.19) | data formatting | bytes 7077888
  85.0 1.1 %copy.19 = f32[3,576,192]{1,2,0:T(8,128)} copy(f32[3,576,192]{1,2,0:T(8,128)S(1)} %bitcast.20) | data formatting | bytes 2654208
  86.1 1.1 %slice-done = s8[4194304]{0:T(1024)(128)(4,1)S(1)} async-done(((s8[5308416]{0:T(1024)(128)(4,1)}), s8[4194304]{0:T(1024)(128)(4,1)S(1)}, s32[]{:S(2)}) %slice-start) | async-done | bytes 4194328
  87.1 0.3 slice-done.1
  87.5 2.5 %slice_bitcast_fusion = (bf16[1536,576]{0,1:T(8,128)(2,1)}, bf16[576,1536]{1,0:T(8,128)(2,1)}, bf16[576,1536]{1,0:T(8,128)(2,1)}) fusion(bf16[3,576,1536]{2,1,0:T(8,128)(2,1)S(1)} %bitcast.22), kind=kLoop, calls=%fused_computation | loop fusion | bytes 10616832 | tf_op jit(solution)/shard_map/transpose | solution.py:477
  90.0 4.1 %copy.20 = f32[1,3,576,1536]{3,2,1,0:T(8,128)} copy(f32[1,3,576,1536]{3,2,1,0:T(8,128)S(1)} %bitcast.18) | data formatting | bytes 21233664
  (1 shorter events, 0.0 us)
Async XLA Ops:
  83.1 4.0 %slice-start = ((s8[5308416]{0:T(1024)(128)(4,1)}), s8[4194304]{0:T(1024)(128)(4,1)S(1)}, s32[]{:S(2)}) async-start(s8[5308416]{0:T(1024)(128)(4,1)} %bitcast.21), calls=%async_computation | async-start | bytes 8388608
  83.2 4.3 %slice-start.1 = ((s8[5308416]{0:T(1024)(128)(4,1)}), s8[1114112]{0:T(1024)(128)(4,1)S(1)}, s32[]{:S(2)}) async-start(s8[5308416]{0:T(1024)(128)(4,1)} %bitcast.21), calls=%async_computation.1 | async-start | bytes 2228224

commit v6 on v5

--- a/solution.py
+++ b/solution.py
@@ -25,9 +25,10 @@
 NTD = (((1,), (1,)), ((), ()))
 
 STEPS = {
-    'AX': (0, 5, 7), 'AY': (0, 1, 2), 'BX': (7, 10, 13), 'BY': (5, 6, 8), 'CX': (9, 13, 15), 'CY': (8, 11, 14),
-    'W1': (3,), 'WZ': (6,), 'WDA': (7,), 'WDB': (9,), 'W3': (16,), 'V': (13,), 'V1': (18, 20, 22),
-    'D0': (11, 15, 17), 'D1': (10, 13, 16), 'E0': (15, 19, 22), 'E1': (13, 17, 20),
+    'AX': (4, 5, 7), 'AY': (0, 1, 2), 'BX': (7, 10, 12), 'BY': (5, 6, 8), 'CX': (9, 12, 14), 'CY': (8, 11, 13),
+    'W1': (3,), 'WZ': (7,), 'WDA': (7,), 'WDB': (9,), 'W3': (16,), 'V': (13,), 'V1': (18, 19, 21), 'V2': (22, 23),
+    'D0': (11, 14, 16), 'D1': (10, 13, 15), 'E0': (15, 18, 21), 'E1': (13, 16, 20),
+    'F0': (18, 21, 24), 'F1': (16, 19, 23),
 }
 
 
@@ -65,7 +66,7 @@
                 pltpu.make_async_copy(dyt.at[:, cols], ys.at[t], s_tok.at[1, t]))
 
     def g_tile(o):
-        return jnp.where(o == 0, 0, jnp.where(o < 4, o + 2, o - 3))
+        return jnp.where(o < 3, o + 3, o - 3)
 
     def gload(n):
         own_half = n >= 6
@@ -154,9 +155,8 @@
 
     for c in to_pair:
         c.start()
-    for t in range(NT):
-        for c in tok(t):
-            c.start()
+    for c in tok(0):
+        c.start()
 
     def send_half(n, _):
         i = g_tile(n)
@@ -176,9 +176,12 @@
     w_x.start()
     w_y.start()
     lax.fori_loop(2, 6, send_half, 0)
+    for t in range(1, NT):
+        for c in tok(t):
+            c.start()
 
     def own_tile(i):
-        n = 6 + (0, 4, 5, 1, 2, 3)[i]
+        n = 6 + (3, 4, 5, 0, 1, 2)[i]
         gload(n).wait()
         to_partner(i).wait_recv()
         for q in range(4):
@@ -240,6 +243,12 @@
             z_out(i).start()
             t_pair(i).start()
 
+    def stage_f(i):
+        @pl.when(at_end)
+        def _():
+            z_out(i).wait_recv()
+            t_pair(i).start()
+
     def v_start():
         for m in range(3):
             local_shards[3 + m].wait()
@@ -282,11 +291,11 @@
         'AX': stage_ax, 'AY': stage_ay, 'BX': stage_bx, 'BY': stage_by,
         'CX': stage_c, 'CY': lambda j: stage_c(3 + j),
         'D0': stage_d, 'D1': lambda j: stage_d(3 + j), 'E0': stage_e, 'E1': lambda j: stage_e(3 + j),
-        'V': lambda j: v_start(), 'V1': v_1,
+        'F0': stage_f, 'F1': lambda j: stage_f(3 + j), 'V': lambda j: v_start(), 'V1': v_1, 'V2': v_2,
         'W1': lambda j: w_1(), 'WZ': lambda j: w_z(), 'WDA': lambda j: w_da.start(), 'WDB': lambda j: w_db.start(),
         'W3': lambda j: w_3(),
     }
-    order = ('W1', 'WZ', 'W3', 'BX', 'BY', 'AX', 'AY', 'CX', 'CY', 'D0', 'D1', 'E0', 'E1', 'WDA', 'WDB', 'V', 'V1')
+    order = ('W1', 'WZ', 'W3', 'BX', 'BY', 'AX', 'AY', 'CX', 'CY', 'D0', 'D1', 'E0', 'E1', 'F0', 'F1', 'WDA', 'WDB', 'V', 'V1', 'V2')
 
     def tick(step, steps):
         for name in order:
@@ -380,6 +389,7 @@
 
     lax.fori_loop(0, 11, two_steps, 0)
     half_step(23, (23,), b0, b1)
+    v_2(2)
     backward(23, *b1)
 
     def write_dx(t, _):
@@ -393,13 +403,6 @@
             if n >= 24:
                 stages[name](j)
 
-    for m in range(3):
-        v_2(m)
-    for i in (0, 3, 1, 4, 2, 5):
-        @pl.when(at_end)
-        def _():
-            z_out(i).wait_recv()
-            t_pair(i).start()
     for i in range(6):
         t_pair(i).wait_recv()
 

time: 94.2 us -> 92.7 us (0.984)
  Pallas kernels: 82.5 us -> 80.8 us
    pallas_call x1, Pallas kernels: 82.5 us -> 80.8 us  [step_kernel(): pl.pallas_call(kernel, name='mlp_step', out_shape=(V((D, N), bf), V((3, D...]
where the time goes in v6:
time: 92.7 us; the launch traced here: 92.4 us
  Pallas kernels  80.8 us (87%)
  local copies, waits for them, and re-layouts  10.9 us (12%)
    pallas_call x1, Pallas kernels, step_kernel(): pl.pallas_call(kernel, name='mlp_step', out_shape=(V((D, N), bf), V((3, D...  80.8 us
    unnamed x7, local copies, waits for them, and re-layouts  8.43 us
    transpose x1, local copies, waits for them, and re-layouts, device_step(): return (dxt.T, gs.transpose(0, 2, 1), dw[None], vo[0], vo[1], vo[2].T)  2.48 us

profile of v6, /device:TPU:0, one launch (start us, length us, event | category | flops | bytes accessed | tf_op | source)
XLA Modules:
  0.0 92.4 jit_solution(5843568922361967098)
XLA Ops:
  0.6 80.8 %mlp_step.1 = (bf16[576,3072]{1,0:T(8,128)(2,1)S(1)}, f32[3,576,1536]{2,1,0:T(8,128)S(1)}, bf16[3,576,1536]{2,1,0:T(8,128)(2,1)}, f32[3,192,576]{2,1,0:T(8,128)S(1)}) custom-call(bf16[576,3072]{1,0:T(8,128)(2,1)} %bitcast.24, bf16[576,3072]{1,0:T(8,128)(2,1)} %bitcast.25, bf16[192,576]{1,0:T(8,128)(2,1)} %bitcast.26, bf16[192,576]{1,0:T(8,128)(2,1)} %bitcast.27, ...), custom_call_target="tpu_custom_call" | custom-call | flops 43499999232 | bytes 60000000 | tf_op jit(solution)/shard_map/mlp_step/pallas_call | solution.py:456
  81.4 0.0 slice-start
  81.5 0.0 slice-start.1
  81.5 1.8 %copy.18 = bf16[3072,576]{0,1:T(8,128)(2,1)} copy(bf16[3072,576]{0,1:T(8,128)(2,1)S(1)} %bitcast.19) | data formatting | bytes 7077888
  83.3 1.1 %copy.19 = f32[3,576,192]{1,2,0:T(8,128)} copy(f32[3,576,192]{1,2,0:T(8,128)S(1)} %bitcast.20) | data formatting | bytes 2654208
  84.4 1.1 %slice-done = s8[4194304]{0:T(1024)(128)(4,1)S(1)} async-done(((s8[5308416]{0:T(1024)(128)(4,1)}), s8[4194304]{0:T(1024)(128)(4,1)S(1)}, s32[]{:S(2)}) %slice-start) | async-done | bytes 4194328
  85.4 0.3 slice-done.1
  85.8 2.5 %slice_bitcast_fusion = (bf16[1536,576]{0,1:T(8,128)(2,1)}, bf16[576,1536]{1,0:T(8,128)(2,1)}, bf16[576,1536]{1,0:T(8,128)(2,1)}) fusion(bf16[3,576,1536]{2,1,0:T(8,128)(2,1)S(1)} %bitcast.22), kind=kLoop, calls=%fused_computation | loop fusion | bytes 10616832 | tf_op jit(solution)/shard_map/transpose | solution.py:480
  88.3 4.1 %copy.20 = f32[1,3,576,1536]{3,2,1,0:T(8,128)} copy(f32[1,3,576,1536]{3,2,1,0:T(8,128)S(1)} %bitcast.18) | data formatting | bytes 21233664
  (1 shorter events, 0.0 us)
Async XLA Ops:
  81.4 4.0 %slice-start = ((s8[5308416]{0:T(1024)(128)(4,1)}), s8[4194304]{0:T(1024)(128)(4,1)S(1)}, s32[]{:S(2)}) async-start(s8[5308416]{0:T(1024)(128)(4,1)} %bitcast.21), calls=%async_computation | async-start | bytes 8388608
  81.5 4.3 %slice-start.1 = ((s8[5308416]{0:T(1024)(128)(4,1)}), s8[1114112]{0:T(1024)(128)(4,1)S(1)}, s32[]{:S(2)}) async-start(s8[5308416]{0:T(1024)(128)(4,1)} %bitcast.21), calls=%async_computation.1 | async-start | bytes 2228224

commit v7 on v6

--- a/solution.py
+++ b/solution.py
@@ -26,7 +26,7 @@
 
 STEPS = {
     'AX': (4, 5, 7), 'AY': (0, 1, 2), 'BX': (7, 10, 12), 'BY': (5, 6, 8), 'CX': (9, 12, 14), 'CY': (8, 11, 13),
-    'W1': (3,), 'WZ': (7,), 'WDA': (7,), 'WDB': (9,), 'W3': (16,), 'V': (13,), 'V1': (18, 19, 21), 'V2': (22, 23),
+    'W1': (4,), 'WZ': (7,), 'WDA': (7,), 'WDB': (9,), 'W3': (16,), 'V': (13,), 'V1': (18, 19, 21), 'V2': (22, 23),
     'D0': (11, 14, 16), 'D1': (10, 13, 15), 'E0': (15, 18, 21), 'E1': (13, 16, 20),
     'F0': (18, 21, 24), 'F1': (16, 19, 23),
 }
@@ -37,9 +37,9 @@
 
 
 def kernel(xt, dyt, w1, w3, w2, v1, v3, v2, g, dxt, dw, vo, gs,
-           ys, pair, blk, vblk, wt, dxa, dab0, hb0, dab1, hb1,
+           ys, pair, blk, wt, dxa, dab0, hb0, dab1, hb1,
            gf, gb, gp, r1, r2, zb, z2, zs, tp,
-           s_tok, s_loc, s_g, s_vo, ss, rs):
+           s_tok, s_loc, s_g, ss, rs):
     xs = dxt
     z = lax.axis_index('dp')
     y = lax.axis_index('col')
@@ -114,12 +114,11 @@
     w_db = rcopy(11, blk.at[2, qb, :], blk.at[3, qb, :], xn)
     w_f3 = rcopy(12, blk.at[3, half, :], blk.at[3, half, :], partner)
 
-    v_own = pltpu.make_async_copy(vblk, vo.at[:, :, blkcols(0, 0)], s_vo)
     def v_copies(m):
         n = 66 + 7 * m
         q0, q1, q2, q3 = blkcols(0, 0), blkcols(1, 0), blkcols(0, 1), blkcols(1, 1)
-        return (rcopy(n, vblk.at[m, half, :], vo.at[m, half, q0], xn),
-                rcopy(n + 1, vblk.at[m, half, :], vo.at[m, half, q0], yn),
+        return (rcopy(n, vo.at[m, half, q0], vo.at[m, half, q0], xn),
+                rcopy(n + 1, vo.at[m, half, q0], vo.at[m, half, q0], yn),
                 rcopy(n + 2, vo.at[m, half, q1], vo.at[m, half, q1], partner),
                 rcopy(n + 3, vo.at[m, half, q2], vo.at[m, half, q2], partner),
                 rcopy(n + 4, vo.at[m, qa, q1], vo.at[m, qa, q1], yn),
@@ -249,14 +248,16 @@
             z_out(i).wait_recv()
             t_pair(i).start()
 
-    def v_start():
+    def v_turn():
         for m in range(3):
             local_shards[3 + m].wait()
             to_pair[3 + m].wait_recv()
-            vblk[m] = pair[1, m].T
+            vo[m, :, blkcols(0, 0)] = pair[1, m].T
+
+    def v_start():
+        for m in range(3):
             v_copies(m)[0].start()
             v_copies(m)[1].start()
-        v_own.start()
 
     def w_1():
         w_y.wait_recv()
@@ -312,10 +313,13 @@
         return pl.ds(pl.multiple_of(q * FC, FC), FC)
 
     def head(c):
+        dw[:, :, dw_cols(c)] = jnp.zeros((3, D, FC), jnp.float32)
+
         @pl.when(c == 1)
         def _():
             w_x.wait_recv()
             w_f1.start()
+            v_turn()
             w_f1.wait_recv()
 
         @pl.when(c == 2)
@@ -328,9 +332,8 @@
             w_f3.wait_recv()
 
         for m in range(3):
-            wt[m * FC:(m + 1) * FC, :] = blk[c, :, m * FC:(m + 1) * FC].T
-
-        dw[:, :, dw_cols(c)] = jnp.zeros((3, D, FC), jnp.float32)
+            rows = slice(m * FC, (m + 1) * FC)
+            wt[rows, :] = pair[0, m] if isinstance(c, int) else blk[c, :, rows].T
 
     def first_touch(t):
         for cp in tok(t):
@@ -417,7 +420,6 @@
                 full = jnp.concatenate(tiles, axis=0).T
                 gs[m] = full[kk * SH:(kk + 1) * SH]
 
-    v_own.wait()
     for i in range(6):
         t_pair(i).wait_send()
         to_partner(i).wait_send()
@@ -456,19 +458,19 @@
     return pl.pallas_call(
         kernel,
         name='mlp_step',
-        out_shape=(V((D, N), bf), V((3, D, F), f32), jax.ShapeDtypeStruct((3, D, F), bf), V((3, SH, D), f32)),
+        out_shape=(V((D, N), bf), V((3, D, F), f32), V((3, D, F), bf), V((3, SH, D), f32)),
         in_specs=[any_spec] * 9,
-        out_specs=(vmem, vmem, any_spec, vmem),
+        out_specs=(vmem,) * 4,
         scratch_shapes=[
-            V((NT, D, T), bf), V((2, 3, FC, D), bf), V((4, D, 3 * FC), bf), V((3, D, FC), bf),
+            V((NT, D, T), bf), V((2, 3, FC, D), bf), V((4, D, 3 * FC), bf),
             V((3 * FC, D), bf), V((NT, D, T), f32),
             V((2 * FC, T), bf), V((FC, T), bf), V((2 * FC, T), bf), V((FC, T), bf),
             V((4, RT, F), f32), V((6, 4, RT, FC), bf), V((6, 4, RT, FC), bf), V((6, 2, RT, FC), bf),
             V((6, RT, FC), bf), V((6, RT, FC), bf), V((6, RT, FC), f32), V((6, RT, FC), f32), V((6, RT, FC), f32),
-            dma((2, NT)), dma((6,)), dma((4,)), dma, dma((93,)), dma((93,)),
+            dma((2, NT)), dma((6,)), dma((4,)), dma((93,)), dma((93,)),
         ],
         compiler_params=pltpu.CompilerParams(
-            collective_id=0, has_side_effects=True, vmem_limit_bytes=50_800_000),
+            collective_id=0, has_side_effects=True, vmem_limit_bytes=45_500_000),
         cost_estimate=pl.CostEstimate(flops=43_500_000_000, bytes_accessed=60_000_000, transcendentals=4_718_592),
     )(xt, dyt, w1, w3, w2, v1, v3, v2, g)
 

time: 92.7 us -> 90.6 us (0.977)
  local copies, waits for them, and re-layouts: 10.9 us -> 9.52 us
    unnamed x7 -> x3, local copies, waits for them, and re-layouts: 8.43 us -> 7.03 us
where the time goes in v7:
time: 90.6 us; the launch traced here: 90.4 us
  Pallas kernels  80.3 us (89%)
  local copies, waits for them, and re-layouts  9.52 us (11%)
    pallas_call x1, Pallas kernels, step_kernel(): pl.pallas_call(kernel, name='mlp_step', out_shape=(V((D, N), bf), V((3, D...  80.3 us
    unnamed x3, local copies, waits for them, and re-layouts  7.03 us
    transpose x1, local copies, waits for them, and re-layouts, device_step(): return (dxt.T, gs.transpose(0, 2, 1), dw[None], vo[0], vo[1], vo[2].T)  2.48 us

profile of v7, /device:TPU:0, one launch (start us, length us, event | category | flops | bytes accessed | tf_op | source)
XLA Modules:
  0.0 90.4 jit_solution(8875242944203553405)
XLA Ops:
  0.6 80.3 %mlp_step.1 = (bf16[576,3072]{1,0:T(8,128)(2,1)S(1)}, f32[3,576,1536]{2,1,0:T(8,128)S(1)}, bf16[3,576,1536]{2,1,0:T(8,128)(2,1)S(1)}, f32[3,192,576]{2,1,0:T(8,128)S(1)}) custom-call(bf16[576,3072]{1,0:T(8,128)(2,1)} %bitcast.22, bf16[576,3072]{1,0:T(8,128)(2,1)} %bitcast.23, bf16[192,576]{1,0:T(8,128)(2,1)} %bitcast.24, bf16[192,576]{1,0:T(8,128)(2,1)} %bitcast.25, ...), custom_call_target="tpu_custom_call" | custom-call | flops 43499999232 | bytes 60000000 | tf_op jit(solution)/shard_map/mlp_step/pallas_call | solution.py:458
  80.9 1.8 %copy.18 = bf16[3072,576]{0,1:T(8,128)(2,1)} copy(bf16[3072,576]{0,1:T(8,128)(2,1)S(1)} %bitcast.19) | data formatting | bytes 7077888
  82.7 1.1 %copy.19 = f32[3,576,192]{1,2,0:T(8,128)} copy(f32[3,576,192]{1,2,0:T(8,128)S(1)} %bitcast.20) | data formatting | bytes 2654208
  83.8 2.5 %slice_bitcast_fusion = (bf16[1536,576]{0,1:T(8,128)(2,1)}, bf16[576,1536]{1,0:T(8,128)(2,1)}, bf16[576,1536]{1,0:T(8,128)(2,1)}) fusion(bf16[3,576,1536]{2,1,0:T(8,128)(2,1)S(1)} %get-tuple-element.13), kind=kLoop, calls=%fused_computation | loop fusion | bytes 10616832 | tf_op jit(solution)/shard_map/transpose | solution.py:482
  86.3 4.1 %copy.20 = f32[1,3,576,1536]{3,2,1,0:T(8,128)} copy(f32[1,3,576,1536]{3,2,1,0:T(8,128)S(1)} %bitcast.18) | data formatting | bytes 21233664

commit v8 on v7

--- a/solution.py
+++ b/solution.py
@@ -26,7 +26,7 @@
 
 STEPS = {
     'AX': (4, 5, 7), 'AY': (0, 1, 2), 'BX': (7, 10, 12), 'BY': (5, 6, 8), 'CX': (9, 12, 14), 'CY': (8, 11, 13),
-    'W1': (4,), 'WZ': (7,), 'WDA': (7,), 'WDB': (9,), 'W3': (16,), 'V': (13,), 'V1': (18, 19, 21), 'V2': (22, 23),
+    'W1': (4,), 'WX': (5,), 'WZ': (7,), 'WDA': (7,), 'WDB': (9,), 'W3': (16,), 'V': (13,), 'V1': (18, 19, 21), 'V2': (22, 23),
     'D0': (11, 14, 16), 'D1': (10, 13, 15), 'E0': (15, 18, 21), 'E1': (13, 16, 20),
     'F0': (18, 21, 24), 'F1': (16, 19, 23),
 }
@@ -104,10 +104,12 @@
     zo = z % 2
     qm = pl.ds(pl.multiple_of(k * HR + zo * QR, QR), QR)
     qo = pl.ds(pl.multiple_of(k * HR + (1 - zo) * QR, QR), QR)
-    w_x = rcopy(6, blk.at[0, half, :], blk.at[1, half, :], xn)
+    w_xa = rcopy(6, blk.at[0, qa, :], blk.at[1, qa, :], xn)
+    w_xb = rcopy(8, blk.at[0, qb, :], blk.at[1, qb, :], xn)
     w_y = rcopy(7, blk.at[0, qm, :], blk.at[2, qm, :], yn)
     w_zy = rcopy(9, blk.at[2, qm, :], blk.at[2, qm, :], zp)
-    w_f1 = rcopy(62, blk.at[1, half, :], blk.at[1, half, :], partner)
+    w_f1a = rcopy(62, blk.at[1, qa, :], blk.at[1, qa, :], partner)
+    w_f1b = rcopy(63, blk.at[1, qb, :], blk.at[1, qb, :], partner)
     w_f2a = rcopy(64, blk.at[2, qm, :], blk.at[2, qm, :], partner)
     w_f2b = rcopy(65, blk.at[2, qo, :], blk.at[2, qo, :], partner)
     w_da = rcopy(10, blk.at[1, qa, :], blk.at[3, qa, :], yn)
@@ -172,7 +174,8 @@
         local_shards[m].wait()
         to_pair[m].wait_recv()
         blk[0, :, m * FC:(m + 1) * FC] = pair[0, m].T
-    w_x.start()
+    w_xa.start()
+    w_xb.start()
     w_y.start()
     lax.fori_loop(2, 6, send_half, 0)
     for t in range(1, NT):
@@ -264,6 +267,10 @@
         w_zy.start()
         w_f2a.start()
 
+    def w_xf():
+        w_xa.wait_recv()
+        w_f1a.start()
+
     def w_z():
         w_zy.wait_recv()
         w_f2b.start()
@@ -293,10 +300,10 @@
         'CX': stage_c, 'CY': lambda j: stage_c(3 + j),
         'D0': stage_d, 'D1': lambda j: stage_d(3 + j), 'E0': stage_e, 'E1': lambda j: stage_e(3 + j),
         'F0': stage_f, 'F1': lambda j: stage_f(3 + j), 'V': lambda j: v_start(), 'V1': v_1, 'V2': v_2,
-        'W1': lambda j: w_1(), 'WZ': lambda j: w_z(), 'WDA': lambda j: w_da.start(), 'WDB': lambda j: w_db.start(),
+        'W1': lambda j: w_1(), 'WX': lambda j: w_xf(), 'WZ': lambda j: w_z(), 'WDA': lambda j: w_da.start(), 'WDB': lambda j: w_db.start(),
         'W3': lambda j: w_3(),
     }
-    order = ('W1', 'WZ', 'W3', 'BX', 'BY', 'AX', 'AY', 'CX', 'CY', 'D0', 'D1', 'E0', 'E1', 'F0', 'F1', 'WDA', 'WDB', 'V', 'V1', 'V2')
+    order = ('W1', 'WX', 'WZ', 'W3', 'BX', 'BY', 'AX', 'AY', 'CX', 'CY', 'D0', 'D1', 'E0', 'E1', 'F0', 'F1', 'WDA', 'WDB', 'V', 'V1', 'V2')
 
     def tick(step, steps):
         for name in order:
@@ -317,10 +324,11 @@
 
         @pl.when(c == 1)
         def _():
-            w_x.wait_recv()
-            w_f1.start()
+            w_xb.wait_recv()
+            w_f1b.start()
             v_turn()
-            w_f1.wait_recv()
+            w_f1a.wait_recv()
+            w_f1b.wait_recv()
 
         @pl.when(c == 2)
         def _():
@@ -440,7 +448,7 @@
         second_y(j).wait_send()
     for c in to_pair:
         c.wait_send()
-    for c in (w_x, w_y, w_zy, w_f1, w_f2a, w_f2b, w_da, w_db, w_f3):
+    for c in (w_xa, w_xb, w_y, w_zy, w_f1a, w_f1b, w_f2a, w_f2b, w_da, w_db, w_f3):
         c.wait_send()
     for m in range(3):
         for c in v_copies(m):

time: 90.6 us -> 90.6 us (level)
  no operation moved by 1% of the time
where the time goes in v8:
time: 90.6 us; the launch traced here: 90.4 us
  Pallas kernels  80.3 us (89%)
  local copies, waits for them, and re-layouts  9.52 us (11%)
    pallas_call x1, Pallas kernels, step_kernel(): pl.pallas_call(kernel, name='mlp_step', out_shape=(V((D, N), bf), V((3, D...  80.3 us
    unnamed x3, local copies, waits for them, and re-layouts  7.03 us
    transpose x1, local copies, waits for them, and re-layouts, device_step(): return (dxt.T, gs.transpose(0, 2, 1), dw[None], vo[0], vo[1], vo[2].T)  2.48 us

profile of v8, /device:TPU:0, one launch (start us, length us, event | category | flops | bytes accessed | tf_op | source)
XLA Modules:
  0.0 90.4 jit_solution(17607534829076806303)
XLA Ops:
  0.6 80.3 %mlp_step.1 = (bf16[576,3072]{1,0:T(8,128)(2,1)S(1)}, f32[3,576,1536]{2,1,0:T(8,128)S(1)}, bf16[3,576,1536]{2,1,0:T(8,128)(2,1)S(1)}, f32[3,192,576]{2,1,0:T(8,128)S(1)}) custom-call(bf16[576,3072]{1,0:T(8,128)(2,1)} %bitcast.22, bf16[576,3072]{1,0:T(8,128)(2,1)} %bitcast.23, bf16[192,576]{1,0:T(8,128)(2,1)} %bitcast.24, bf16[192,576]{1,0:T(8,128)(2,1)} %bitcast.25, ...), custom_call_target="tpu_custom_call" | custom-call | flops 43499999232 | bytes 60000000 | tf_op jit(solution)/shard_map/mlp_step/pallas_call | solution.py:466
  80.9 1.8 %copy.18 = bf16[3072,576]{0,1:T(8,128)(2,1)} copy(bf16[3072,576]{0,1:T(8,128)(2,1)S(1)} %bitcast.19) | data formatting | bytes 7077888
  82.7 1.1 %copy.19 = f32[3,576,192]{1,2,0:T(8,128)} copy(f32[3,576,192]{1,2,0:T(8,128)S(1)} %bitcast.20) | data formatting | bytes 2654208
  83.8 2.5 %slice_bitcast_fusion = (bf16[1536,576]{0,1:T(8,128)(2,1)}, bf16[576,1536]{1,0:T(8,128)(2,1)}, bf16[576,1536]{1,0:T(8,128)(2,1)}) fusion(bf16[3,576,1536]{2,1,0:T(8,128)(2,1)S(1)} %get-tuple-element.13), kind=kLoop, calls=%fused_computation | loop fusion | bytes 10616832 | tf_op jit(solution)/shard_map/transpose | solution.py:490
  86.3 4.1 %copy.20 = f32[1,3,576,1536]{3,2,1,0:T(8,128)} copy(f32[1,3,576,1536]{3,2,1,0:T(8,128)S(1)} %bitcast.18) | data formatting | bytes 21233664
